TPU v7x, 128 devices: a whole 4x4x4 slice. The times are simulated.
128 devices in a mesh: section: 32 (over y, z, core), state: 4 (over x).
Axes of the slice: x: 4, y: 4, z: 4, core: 2. Of those that a mesh axis runs over, the one named last changes fastest.
Arguments:
- initial_state: float32 [32, 1024], P('state'), may hold values from -6 to 6
- state_ref: float32 [768, 32, 1024], P('section', 'state'), may hold values from -6 to 6
- state_weight: float32 [768, 32, 1024], P('section', 'state'), may hold values from 0.2 to 5
- input_matrix: bfloat16 [32, 1024, 512], P('state'), may hold values from -0.25 to 0.25
- kkt_inverse: float32 [512, 512], replicated, may hold values from -1 to 1, as said below
- input_bound: float32 [512], replicated, may hold values from 0.02 to 0.3
Outputs:
- states: float32 [768, 32, 1024], P('section', 'state')
- boxed: float32 [768, 512], P('section')
- dual_vars: float32 [768, 32, 1024], P('section', 'state')
- history: float32 [10, 2], replicated
Inputs may be any that keep to these rules, and one draw needn't show every extreme that they name: `kkt_inverse`: a symmetric matrix.
All inputs are finite; a program needn't handle non-finite values.
Results may differ from a plain program's by a relative error of at most 0.003.
Values may be sent and summed in bfloat16 or wider, within the bound.
A program may use at most 128 MiB of HBM per device.

v0:
```python
import jax
import jax.numpy as jnp
from jax import lax
from jax.sharding import Mesh
from jax.sharding import PartitionSpec as P

GX = 32
GY = 32
GZ = 32
ITERS = 10
SECTION = ("section_0", "section_1", "section_2")
SECTION_STATE = ("section_0", "section_1", "section_2", "state")


diffusion = 0.15
epsilon = 1e-06


def passed_along(value, axis, steps):
    count = lax.axis_size(axis)
    leading, last = (max(0, -steps), min(count, count - steps))
    return lax.ppermute(value, axis, [(source, source + steps) for source in range(leading, last)])


def with_halo(block, sides, width):
    for axis, dim in sides:
        count = lax.axis_size(axis)
        forward = [(i, i + 1) for i in range(count - 1)]
        backward = [(target, source) for source, target in forward]
        low = lax.ppermute(
            lax.slice_in_dim(block, block.shape[dim] - width, None, axis=dim), axis, forward
        )
        high = lax.ppermute(lax.slice_in_dim(block, 0, width, axis=dim), axis, backward)
        block = jnp.concatenate([low, block, high], axis=dim)
    return block


def copy_for_each(x, axis):
    copies = jnp.broadcast_to(x, (lax.axis_size(axis), *x.shape))
    return lax.all_to_all(copies, axis, split_axis=0, concat_axis=0, tiled=True)


def over_copies(x, axis):
    return copy_for_each(x, axis).sum(axis=0)


def by_axis(x, axes):
    for axis in axes:
        x = lax.psum(x, axis)
    return x


def stencil(padded):
    centre = padded[:, 1:-1]
    across = padded[:, 2:] + padded[:, :-2]
    depth = centre.shape[-1]
    flat_pad = jnp.pad(centre, ((0, 0), (0, 0), (GZ, GZ)))
    along_y = flat_pad[:, :, 2 * GZ :] + flat_pad[:, :, : -2 * GZ]
    lower_z = jnp.pad(centre, ((0, 0), (0, 0), (1, 0)))[:, :, :-1]
    upper_z = jnp.pad(centre, ((0, 0), (0, 0), (0, 1)))[:, :, 1:]
    z_index = jnp.arange(depth) % GZ
    along_z = jnp.where(z_index > 0, lower_z, 0.0) + jnp.where(z_index < GZ - 1, upper_z, 0.0)
    return centre + diffusion * (across + along_y + along_z - 6.0 * centre)


def apply_rows(inputs_low, matrix):
    return lax.dot_general(
        inputs_low, matrix, (((1,), (1,)), ((), ())), preferred_element_type=jnp.float32
    )


def local(initial_state, state_ref, state_weight, input_matrix, kkt_inverse, input_bound):
    section_count, planes, plane_size = state_ref.shape
    input_width = input_matrix.shape[2]
    matrix = input_matrix.reshape(planes * plane_size, input_width)
    penalty = float(GX * GY * GZ) / input_width
    is_first = lax.axis_index(SECTION) == 0
    groups = lax.axis_size("state")
    cell_count = section_count * lax.axis_size(SECTION) * GX * GY * GZ
    input_count = section_count * lax.axis_size(SECTION) * input_width
    states = jnp.zeros_like(state_ref)
    dual_vars = jnp.zeros_like(state_ref)
    boxed = jnp.zeros((section_count, input_width), jnp.float32)
    scaled = jnp.zeros((section_count, input_width), jnp.float32)
    primal_sums = []
    gap_sums = []
    for iteration in range(ITERS):
        last_state = passed_along(states[-1], SECTION, 1)
        prior = jnp.where(is_first, initial_state, last_state)
        before = jnp.concatenate([prior[None], states[:-1]], 0)
        moved_prior = stencil(with_halo(before, (("state", 1),), 1))
        target = states - moved_prior + dual_vars
        target_low = target.astype(jnp.bfloat16).reshape(section_count, -1)
        partial_pull = jnp.dot(target_low, matrix, preferred_element_type=jnp.float32)
        pulled = over_copies(partial_pull, "state")
        rhs_rows = pulled + penalty * (boxed - scaled)
        inputs = jnp.dot(rhs_rows, kkt_inverse, precision=lax.Precision.HIGHEST)
        inputs_low = inputs.astype(jnp.bfloat16)
        driven = apply_rows(inputs_low, matrix).reshape(section_count, planes, plane_size)
        defect = target - driven
        following = passed_along(defect[0], SECTION, -1)
        ahead_defect = jnp.concatenate([defect[1:], following[None]], 0)
        back_term = stencil(with_halo(ahead_defect, (("state", 1),), 1))
        updated = (state_weight * state_ref + (states - defect) + back_term + states) / (
            state_weight + 2.0
        )
        primal = updated - moved_prior - driven
        dual_vars = dual_vars + primal
        boxed_new = jnp.clip(inputs + scaled, -input_bound, input_bound)
        box_gap = inputs - boxed_new
        scaled = scaled + box_gap
        boxed = boxed_new
        states = updated
        primal_square = jnp.sum(primal * primal)
        gap_square = jnp.sum(box_gap * box_gap) / groups
        primal_sums.append(primal_square)
        gap_sums.append(gap_square)
    totals = (
        by_axis(jnp.stack(primal_sums), SECTION_STATE),
        by_axis(jnp.stack(gap_sums), SECTION_STATE),
    )
    record = jnp.stack(
        [jnp.sqrt(totals[0] / cell_count + epsilon), jnp.sqrt(totals[1] / input_count + epsilon)], 1
    )
    return (states, boxed, dual_vars, record)


def solution(mesh):
    finer = Mesh(
        mesh.devices.reshape(4, 4, 2, mesh.shape["state"]),
        ("section_0", "section_1", "section_2", "state"),
    )
    return jax.shard_map(
        local,
        mesh=finer,
        in_specs=(
            P("state", None),
            P(SECTION, "state", None),
            P(SECTION, "state", None),
            P("state", None, None),
            P(),
            P(),
        ),
        out_specs=(P(SECTION, "state", None), P(SECTION, None), P(SECTION, "state", None), P()),
        check_vma=False,
    )
```

profile of v0, /device:TPU:0, one launch (start us, length us, event | category | flops | bytes accessed | tf_op | source)
XLA Modules:
  0.0 619.0 jit_solution(17903014731025055805)
XLA Ops:
  5.1 4.6 collective-permute-start.2
  12.9 5.2 convolution_bitcast_fusion.9
  18.1 12.6 %all_to_all.50 = f32[4,24,512]{2,1,0:T(8,128)S(1)} all-to-all(f32[4,24,512]{2,1,0:T(8,128)S(1)} %broadcast_in_dim.281), channel_id=1, replica_groups=mesh['section_0'=4,'section_1'=4,'section_2'=2,'state'=4] {'state'}, dimensions={0} | all-to-all | bytes 393216 | tf_op jit(solution)/shard_map/all_to_all | solution.py:40
  31.4 5.7 fusion.346
  42.2 4.6 collective-permute-start.5
  48.9 3.0 fusion.429
  51.9 4.4 collective-permute-start.6
  59.1 4.6 collective-permute-start.8
  70.4 6.3 %all-to-all-start.1 = ((f32[4,24,512]{2,1,0:T(8,128)}), f32[4,24,512]{2,1,0:T(8,128)}, u32[]{:S(2)}, u32[]{:S(2)}) async-start(f32[4,24,512]{2,1,0:T(8,128)} %broadcast_in_dim.284), calls=%async_computation.1 | async-start | bytes 393216 | tf_op jit(solution)/shard_map/all_to_all | solution.py:40
  76.7 6.5 %all-to-all-done.1 = f32[4,24,512]{2,1,0:T(8,128)} async-done(((f32[4,24,512]{2,1,0:T(8,128)}), f32[4,24,512]{2,1,0:T(8,128)}, u32[]{:S(2)}, u32[]{:S(2)}) %all-to-all-start.1) | async-done | bytes 196640 | tf_op jit(solution)/shard_map/all_to_all | solution.py:40
  85.4 5.7 fusion.344
  96.7 4.6 collective-permute-start.11
  103.4 3.1 multiply_reduce_fusion.8
  106.5 4.3 collective-permute-start.12
  113.2 4.6 collective-permute-start.14
  124.0 12.9 %all_to_all.51 = f32[4,24,512]{2,1,0:T(8,128)} all-to-all(f32[4,24,512]{2,1,0:T(8,128)S(1)} %broadcast_in_dim.287), channel_id=1, replica_groups=mesh['section_0'=4,'section_1'=4,'section_2'=2,'state'=4] {'state'}, dimensions={0} | all-to-all | bytes 393216 | tf_op jit(solution)/shard_map/all_to_all | solution.py:40
  140.1 5.7 fusion.342
  151.5 4.6 collective-permute-start.17
  158.2 3.0 multiply_reduce_fusion.7
  161.3 5.0 collective-permute-start.18
  168.6 4.6 collective-permute-start.20
  179.4 12.5 %all_to_all.52 = f32[4,24,512]{2,1,0:T(8,128)} all-to-all(f32[4,24,512]{2,1,0:T(8,128)S(1)} %broadcast_in_dim.290), channel_id=1, replica_groups=mesh['section_0'=4,'section_1'=4,'section_2'=2,'state'=4] {'state'}, dimensions={0} | all-to-all | bytes 393216 | tf_op jit(solution)/shard_map/all_to_all | solution.py:40
  195.7 5.7 fusion.340
  206.9 4.6 collective-permute-start.23
  213.7 3.1 multiply_reduce_fusion.6
  216.8 4.8 collective-permute-start.24
  224.0 4.6 collective-permute-start.26
  234.9 12.7 %all_to_all.53 = f32[4,24,512]{2,1,0:T(8,128)} all-to-all(f32[4,24,512]{2,1,0:T(8,128)S(1)} %broadcast_in_dim.293), channel_id=1, replica_groups=mesh['section_0'=4,'section_1'=4,'section_2'=2,'state'=4] {'state'}, dimensions={0} | all-to-all | bytes 393216 | tf_op jit(solution)/shard_map/all_to_all | solution.py:40
  250.8 5.7 fusion.338
  262.1 4.6 collective-permute-start.29
  268.9 3.1 multiply_reduce_fusion.5
  272.0 4.2 collective-permute-start.30
  278.6 4.6 collective-permute-start.32
  289.4 12.7 %all_to_all.54 = f32[4,24,512]{2,1,0:T(8,128)} all-to-all(f32[4,24,512]{2,1,0:T(8,128)S(1)} %broadcast_in_dim.296), channel_id=1, replica_groups=mesh['section_0'=4,'section_1'=4,'section_2'=2,'state'=4] {'state'}, dimensions={0} | all-to-all | bytes 393216 | tf_op jit(solution)/shard_map/all_to_all | solution.py:40
  305.9 5.7 fusion.336
  317.2 4.6 collective-permute-start.35
  324.0 3.1 multiply_reduce_fusion.4
  327.1 5.2 collective-permute-start.36
  334.7 4.6 collective-permute-start.38
  345.6 12.6 %all_to_all.55 = f32[4,24,512]{2,1,0:T(8,128)} all-to-all(f32[4,24,512]{2,1,0:T(8,128)S(1)} %broadcast_in_dim.299), channel_id=1, replica_groups=mesh['section_0'=4,'section_1'=4,'section_2'=2,'state'=4] {'state'}, dimensions={0} | all-to-all | bytes 393216 | tf_op jit(solution)/shard_map/all_to_all | solution.py:40
  361.4 5.7 fusion.334
  372.7 4.6 collective-permute-start.41
  379.5 3.1 multiply_reduce_fusion.3
  382.6 5.2 collective-permute-start.42
  390.2 4.6 collective-permute-start.44
  401.0 12.7 %all_to_all.56 = f32[4,24,512]{2,1,0:T(8,128)} all-to-all(f32[4,24,512]{2,1,0:T(8,128)S(1)} %broadcast_in_dim.302), channel_id=1, replica_groups=mesh['section_0'=4,'section_1'=4,'section_2'=2,'state'=4] {'state'}, dimensions={0} | all-to-all | bytes 393216 | tf_op jit(solution)/shard_map/all_to_all | solution.py:40
  417.5 5.7 fusion.332
  428.8 4.6 collective-permute-start.47
  439.2 6.1 collective-permute-start.48
  447.9 4.6 collective-permute-start.50
  459.4 12.6 %all_to_all.57 = f32[4,24,512]{2,1,0:T(8,128)} all-to-all(f32[4,24,512]{2,1,0:T(8,128)S(1)} %broadcast_in_dim.305), channel_id=1, replica_groups=mesh['section_0'=4,'section_1'=4,'section_2'=2,'state'=4] {'state'}, dimensions={0} | all-to-all | bytes 393216 | tf_op jit(solution)/shard_map/all_to_all | solution.py:40
  475.1 5.8 copy_subtract_fusion.1
  486.2 4.6 collective-permute-start.53
  497.1 6.3 %collective-permute-start.54 = (f32[8,1024]{1,0:T(8,128)S(1)}, f32[8,1024]{1,0:T(8,128)S(1)}, u32[]{:S(2)}, u32[]{:S(2)}) collective-permute-start(f32[8,1024]{1,0:T(8,128)S(1)} %slice_bitcast_fusion), channel_id=1, source_target_pairs={{0,4},{4,8},{8,12},{12,16},{16,20},{20,24},{24,28},{28,32},{32,36}... | collective-permute-start | bytes 98312 | tf_op jit(solution)/shard_map/ppermute | solution.py:22
  505.7 4.6 collective-permute-start.56
  516.1 12.3 %all_to_all.58 = f32[4,24,512]{2,1,0:T(8,128)} all-to-all(f32[4,24,512]{2,1,0:T(8,128)S(1)} %broadcast_in_dim.308), channel_id=1, replica_groups=mesh['section_0'=4,'section_1'=4,'section_2'=2,'state'=4] {'state'}, dimensions={0} | all-to-all | bytes 393216 | tf_op jit(solution)/shard_map/all_to_all | solution.py:40
  530.0 3.1 multiply_reduce_fusion.12
  533.1 6.7 %fusion.432 = (f32[24,8,1024]{2,0,1:T(8,128)S(1)}, f32[24,8,1024]{2,0,1:T(8,128)}) fusion(f32[24,8,1024]{2,0,1:T(8,128)} %copy-done.26, bf16[8,1024,512]{2,1,0:T(8,128)(2,1)} %param.9, bf16[24,512]{1,0:T(8,128)(2,1)S(1)} %get-tuple-element.145), kind=kOutput, calls=%fused_computation.773 | convolution fusion | flops 201523200 | bytes 10772480 | tf_op jit(solution)/shard_map/dot_general | solution.py:67
  550.8 4.8 collective-permute-start.59
  558.4 4.2 multiply_reduce_fusion
  564.7 6.3 %stack.85 = f32[10]{0:T(128)S(1)} concatenate(f32[1]{0:T(128)} %bitcast.56, f32[1]{0:T(128)} %bitcast.57, f32[1]{0:T(128)} %bitcast.58, f32[1]{0:T(128)} %bitcast.59, f32[1]{0:T(128)} %bitcast.60, f32[1]{0:T(128)} %bitcast.61, f32[1]{0:T(128)} %bitcast.62, f32[1]{0:T(128)} %bitcast.63, f32[1]{0:T(128)} %bitcast.64, f32[1]{0:T(128)} %bitcast.65), dimensions={0} | concatenate | bytes 80 | tf_op jit(solution)/shard_map/stack | solution.py:119
  572.3 25.2 %all-reduce.63 = (f32[10]{0:T(128)S(1)}, f32[10]{0:T(128)S(1)}) all-reduce(f32[10]{0:T(128)S(1)} %stack.97, f32[10]{0:T(128)S(1)} %stack.85), channel_id=1, replica_groups=mesh['section_0'=4,'section_1'=4,'section_2'=2,'state'=4] {'section_0'}, use_global_device_ids=true, to_apply=%region_34.35 | all-reduce | flops 20 | bytes 160 | tf_op jit(solution)/shard_map/psum | solution.py:49
  597.5 7.7 %all-reduce.62 = (f32[10]{0:T(128)S(1)}, f32[10]{0:T(128)S(1)}) all-reduce(f32[10]{0:T(128)S(1)} %get-tuple-element.32, f32[10]{0:T(128)S(1)} %get-tuple-element.33), channel_id=1, replica_groups=mesh['section_0'=4,'section_1'=4,'section_2'=2,'state'=4] {'section_1'}, use_global_device_ids=true, to_apply=%region_35.36 | all-reduce | flops 20 | bytes 160 | tf_op jit(solution)/shard_map/psum | solution.py:49
  607.7 10.2 %all-reduce.61 = (f32[10]{0:T(128)S(1)}, f32[10]{0:T(128)S(1)}) all-reduce(f32[10]{0:T(128)S(1)} %get-tuple-element.34, f32[10]{0:T(128)S(1)} %get-tuple-element.35), channel_id=1, replica_groups=mesh['section_0'=4,'section_1'=4,'section_2'=2,'state'=4] {'state'}, use_global_device_ids=true, to_apply=%region_37.38 | all-reduce | flops 20 | bytes 160 | tf_op jit(solution)/shard_map/psum | solution.py:49
  (419 shorter events, 204.4 us)
Async XLA Ops:
  0.6 30.1 %copy-start = (f32[512,512]{1,0:T(8,128)S(1)}, f32[512,512]{1,0:T(8,128)}, u32[]{:S(2)}) copy-start(f32[512,512]{1,0:T(8,128)} %param.10) | copy-start | bytes 3145732
  0.7 2.3 collective-permute-start
  3.8 6.5 %collective-permute-start.1 = (f32[24,1,1024]{2,1,0:T(1,128)S(1)}, f32[24,1,1024]{2,1,0:T(1,128)S(1)}, u32[]{:S(2)}, u32[]{:S(2)}) collective-permute-start(f32[24,1,1024]{2,1,0:T(1,128)S(1)} %get-tuple-element.131), channel_id=1, source_target_pairs={{1,0},{2,1},{3,2},{5,4},{6,5},{7,6},{9,8},{10,9},{11,10},{13,12},{... | collective-permute-start | bytes 294920 | tf_op jit(solution)/shard_map/ppermute | solution.py:33
  5.1 6.9 %collective-permute-start.2 = (f32[24,1,1024]{2,1,0:T(1,128)S(1)}, f32[24,1,1024]{2,1,0:T(1,128)S(1)}, u32[]{:S(2)}, u32[]{:S(2)}) collective-permute-start(f32[24,1,1024]{2,1,0:T(1,128)S(1)} %get-tuple-element.132), channel_id=1, source_target_pairs={{0,1},{1,2},{2,3},{4,5},{5,6},{6,7},{8,9},{9,10},{10,11},{12,13},{... | collective-permute-start | bytes 294920 | tf_op jit(solution)/shard_map/ppermute | solution.py:30
  12.9 24.2 %copy-start.28 = (f32[24,8,1024]{2,1,0:T(8,128)}, f32[24,8,1024]{2,1,0:T(8,128)S(1)}, u32[]{:S(2)}) copy-start(f32[24,8,1024]{2,1,0:T(8,128)S(1)} %get-tuple-element.86) | copy-start | bytes 2359300
  37.6 3.1 collective-permute-start.3
  40.9 6.5 %collective-permute-start.4 = (f32[24,1,1024]{2,1,0:T(1,128)S(1)}, f32[24,1,1024]{2,1,0:T(1,128)S(1)}, u32[]{:S(2)}, u32[]{:S(2)}) collective-permute-start(f32[24,1,1024]{2,1,0:T(1,128)S(1)} %get-tuple-element.127), channel_id=1, source_target_pairs={{1,0},{2,1},{3,2},{5,4},{6,5},{7,6},{9,8},{10,9},{11,10},{13,12},{... | collective-permute-start | bytes 294920 | tf_op jit(solution)/shard_map/ppermute | solution.py:33
  42.2 6.8 %collective-permute-start.5 = (f32[24,1,1024]{2,1,0:T(1,128)S(1)}, f32[24,1,1024]{2,1,0:T(1,128)S(1)}, u32[]{:S(2)}, u32[]{:S(2)}) collective-permute-start(f32[24,1,1024]{2,1,0:T(1,128)S(1)} %get-tuple-element.128), channel_id=1, source_target_pairs={{0,1},{1,2},{2,3},{4,5},{5,6},{6,7},{8,9},{9,10},{10,11},{12,13},{... | collective-permute-start | bytes 294920 | tf_op jit(solution)/shard_map/ppermute | solution.py:30
  51.9 5.6 collective-permute-start.6
  57.6 6.8 %collective-permute-start.7 = (f32[24,1,1024]{2,1,0:T(1,128)S(1)}, f32[24,1,1024]{2,1,0:T(1,128)S(1)}, u32[]{:S(2)}, u32[]{:S(2)}) collective-permute-start(f32[24,1,1024]{2,1,0:T(1,128)S(1)} %get-tuple-element.123), channel_id=1, source_target_pairs={{1,0},{2,1},{3,2},{5,4},{6,5},{7,6},{9,8},{10,9},{11,10},{13,12},{... | collective-permute-start | bytes 294920 | tf_op jit(solution)/shard_map/ppermute | solution.py:33
  59.1 7.1 %collective-permute-start.8 = (f32[24,1,1024]{2,1,0:T(1,128)S(1)}, f32[24,1,1024]{2,1,0:T(1,128)S(1)}, u32[]{:S(2)}, u32[]{:S(2)}) collective-permute-start(f32[24,1,1024]{2,1,0:T(1,128)S(1)} %get-tuple-element.124), channel_id=1, source_target_pairs={{0,1},{1,2},{2,3},{4,5},{5,6},{6,7},{8,9},{9,10},{10,11},{12,13},{... | collective-permute-start | bytes 294920 | tf_op jit(solution)/shard_map/ppermute | solution.py:30
  70.4 12.8 %all-to-all-start.1 = ((f32[4,24,512]{2,1,0:T(8,128)}), f32[4,24,512]{2,1,0:T(8,128)}, u32[]{:S(2)}, u32[]{:S(2)}) async-start(f32[4,24,512]{2,1,0:T(8,128)} %broadcast_in_dim.284), calls=%async_computation.1 | async-start | bytes 393216 | tf_op jit(solution)/shard_map/all_to_all | solution.py:40
  92.2 3.1 collective-permute-start.9
  95.4 6.5 %collective-permute-start.10 = (f32[24,1,1024]{2,1,0:T(1,128)S(1)}, f32[24,1,1024]{2,1,0:T(1,128)S(1)}, u32[]{:S(2)}, u32[]{:S(2)}) collective-permute-start(f32[24,1,1024]{2,1,0:T(1,128)S(1)} %get-tuple-element.121), channel_id=1, source_target_pairs={{1,0},{2,1},{3,2},{5,4},{6,5},{7,6},{9,8},{10,9},{11,10},{13,12},{... | collective-permute-start | bytes 294920 | tf_op jit(solution)/shard_map/ppermute | solution.py:33
  96.7 6.8 %collective-permute-start.11 = (f32[24,1,1024]{2,1,0:T(1,128)S(1)}, f32[24,1,1024]{2,1,0:T(1,128)S(1)}, u32[]{:S(2)}, u32[]{:S(2)}) collective-permute-start(f32[24,1,1024]{2,1,0:T(1,128)S(1)} %get-tuple-element.122), channel_id=1, source_target_pairs={{0,1},{1,2},{2,3},{4,5},{5,6},{6,7},{8,9},{9,10},{10,11},{12,13},{... | collective-permute-start | bytes 294920 | tf_op jit(solution)/shard_map/ppermute | solution.py:30
  106.5 5.2 collective-permute-start.12
  111.8 6.8 %collective-permute-start.13 = (f32[24,1,1024]{2,1,0:T(1,128)S(1)}, f32[24,1,1024]{2,1,0:T(1,128)S(1)}, u32[]{:S(2)}, u32[]{:S(2)}) collective-permute-start(f32[24,1,1024]{2,1,0:T(1,128)S(1)} %get-tuple-element.119), channel_id=1, source_target_pairs={{1,0},{2,1},{3,2},{5,4},{6,5},{7,6},{9,8},{10,9},{11,10},{13,12},{... | collective-permute-start | bytes 294920 | tf_op jit(solution)/shard_map/ppermute | solution.py:33
  113.2 7.1 %collective-permute-start.14 = (f32[24,1,1024]{2,1,0:T(1,128)S(1)}, f32[24,1,1024]{2,1,0:T(1,128)S(1)}, u32[]{:S(2)}, u32[]{:S(2)}) collective-permute-start(f32[24,1,1024]{2,1,0:T(1,128)S(1)} %get-tuple-element.120), channel_id=1, source_target_pairs={{0,1},{1,2},{2,3},{4,5},{5,6},{6,7},{8,9},{9,10},{10,11},{12,13},{... | collective-permute-start | bytes 294920 | tf_op jit(solution)/shard_map/ppermute | solution.py:30
  146.9 3.1 collective-permute-start.15
  150.2 6.5 %collective-permute-start.16 = (f32[24,1,1024]{2,1,0:T(1,128)S(1)}, f32[24,1,1024]{2,1,0:T(1,128)S(1)}, u32[]{:S(2)}, u32[]{:S(2)}) collective-permute-start(f32[24,1,1024]{2,1,0:T(1,128)S(1)} %get-tuple-element.117), channel_id=1, source_target_pairs={{1,0},{2,1},{3,2},{5,4},{6,5},{7,6},{9,8},{10,9},{11,10},{13,12},{... | collective-permute-start | bytes 294920 | tf_op jit(solution)/shard_map/ppermute | solution.py:33
  151.5 6.8 %collective-permute-start.17 = (f32[24,1,1024]{2,1,0:T(1,128)S(1)}, f32[24,1,1024]{2,1,0:T(1,128)S(1)}, u32[]{:S(2)}, u32[]{:S(2)}) collective-permute-start(f32[24,1,1024]{2,1,0:T(1,128)S(1)} %get-tuple-element.118), channel_id=1, source_target_pairs={{0,1},{1,2},{2,3},{4,5},{5,6},{6,7},{8,9},{9,10},{10,11},{12,13},{... | collective-permute-start | bytes 294920 | tf_op jit(solution)/shard_map/ppermute | solution.py:30
  161.3 5.8 collective-permute-start.18
  167.2 6.9 %collective-permute-start.19 = (f32[24,1,1024]{2,1,0:T(1,128)S(1)}, f32[24,1,1024]{2,1,0:T(1,128)S(1)}, u32[]{:S(2)}, u32[]{:S(2)}) collective-permute-start(f32[24,1,1024]{2,1,0:T(1,128)S(1)} %get-tuple-element.115), channel_id=1, source_target_pairs={{1,0},{2,1},{3,2},{5,4},{6,5},{7,6},{9,8},{10,9},{11,10},{13,12},{... | collective-permute-start | bytes 294920 | tf_op jit(solution)/shard_map/ppermute | solution.py:33
  168.6 7.2 %collective-permute-start.20 = (f32[24,1,1024]{2,1,0:T(1,128)S(1)}, f32[24,1,1024]{2,1,0:T(1,128)S(1)}, u32[]{:S(2)}, u32[]{:S(2)}) collective-permute-start(f32[24,1,1024]{2,1,0:T(1,128)S(1)} %get-tuple-element.116), channel_id=1, source_target_pairs={{0,1},{1,2},{2,3},{4,5},{5,6},{6,7},{8,9},{9,10},{10,11},{12,13},{... | collective-permute-start | bytes 294920 | tf_op jit(solution)/shard_map/ppermute | solution.py:30
  202.4 3.1 collective-permute-start.21
  205.6 6.5 %collective-permute-start.22 = (f32[24,1,1024]{2,1,0:T(1,128)S(1)}, f32[24,1,1024]{2,1,0:T(1,128)S(1)}, u32[]{:S(2)}, u32[]{:S(2)}) collective-permute-start(f32[24,1,1024]{2,1,0:T(1,128)S(1)} %get-tuple-element.113), channel_id=1, source_target_pairs={{1,0},{2,1},{3,2},{5,4},{6,5},{7,6},{9,8},{10,9},{11,10},{13,12},{... | collective-permute-start | bytes 294920 | tf_op jit(solution)/shard_map/ppermute | solution.py:33
  206.9 6.8 %collective-permute-start.23 = (f32[24,1,1024]{2,1,0:T(1,128)S(1)}, f32[24,1,1024]{2,1,0:T(1,128)S(1)}, u32[]{:S(2)}, u32[]{:S(2)}) collective-permute-start(f32[24,1,1024]{2,1,0:T(1,128)S(1)} %get-tuple-element.114), channel_id=1, source_target_pairs={{0,1},{1,2},{2,3},{4,5},{5,6},{6,7},{8,9},{9,10},{10,11},{12,13},{... | collective-permute-start | bytes 294920 | tf_op jit(solution)/shard_map/ppermute | solution.py:30
  216.8 5.6 collective-permute-start.24
  222.6 6.9 %collective-permute-start.25 = (f32[24,1,1024]{2,1,0:T(1,128)S(1)}, f32[24,1,1024]{2,1,0:T(1,128)S(1)}, u32[]{:S(2)}, u32[]{:S(2)}) collective-permute-start(f32[24,1,1024]{2,1,0:T(1,128)S(1)} %get-tuple-element.111), channel_id=1, source_target_pairs={{1,0},{2,1},{3,2},{5,4},{6,5},{7,6},{9,8},{10,9},{11,10},{13,12},{... | collective-permute-start | bytes 294920 | tf_op jit(solution)/shard_map/ppermute | solution.py:33
  224.0 7.2 %collective-permute-start.26 = (f32[24,1,1024]{2,1,0:T(1,128)S(1)}, f32[24,1,1024]{2,1,0:T(1,128)S(1)}, u32[]{:S(2)}, u32[]{:S(2)}) collective-permute-start(f32[24,1,1024]{2,1,0:T(1,128)S(1)} %get-tuple-element.112), channel_id=1, source_target_pairs={{0,1},{1,2},{2,3},{4,5},{5,6},{6,7},{8,9},{9,10},{10,11},{12,13},{... | collective-permute-start | bytes 294920 | tf_op jit(solution)/shard_map/ppermute | solution.py:30
  257.6 3.1 collective-permute-start.27
  260.8 6.5 %collective-permute-start.28 = (f32[24,1,1024]{2,1,0:T(1,128)S(1)}, f32[24,1,1024]{2,1,0:T(1,128)S(1)}, u32[]{:S(2)}, u32[]{:S(2)}) collective-permute-start(f32[24,1,1024]{2,1,0:T(1,128)S(1)} %get-tuple-element.109), channel_id=1, source_target_pairs={{1,0},{2,1},{3,2},{5,4},{6,5},{7,6},{9,8},{10,9},{11,10},{13,12},{... | collective-permute-start | bytes 294920 | tf_op jit(solution)/shard_map/ppermute | solution.py:33
  262.1 6.8 %collective-permute-start.29 = (f32[24,1,1024]{2,1,0:T(1,128)S(1)}, f32[24,1,1024]{2,1,0:T(1,128)S(1)}, u32[]{:S(2)}, u32[]{:S(2)}) collective-permute-start(f32[24,1,1024]{2,1,0:T(1,128)S(1)} %get-tuple-element.110), channel_id=1, source_target_pairs={{0,1},{1,2},{2,3},{4,5},{5,6},{6,7},{8,9},{9,10},{10,11},{12,13},{... | collective-permute-start | bytes 294920 | tf_op jit(solution)/shard_map/ppermute | solution.py:30
  272.0 5.1 collective-permute-start.30
  277.2 6.9 %collective-permute-start.31 = (f32[24,1,1024]{2,1,0:T(1,128)S(1)}, f32[24,1,1024]{2,1,0:T(1,128)S(1)}, u32[]{:S(2)}, u32[]{:S(2)}) collective-permute-start(f32[24,1,1024]{2,1,0:T(1,128)S(1)} %get-tuple-element.107), channel_id=1, source_target_pairs={{1,0},{2,1},{3,2},{5,4},{6,5},{7,6},{9,8},{10,9},{11,10},{13,12},{... | collective-permute-start | bytes 294920 | tf_op jit(solution)/shard_map/ppermute | solution.py:33
  278.6 7.2 %collective-permute-start.32 = (f32[24,1,1024]{2,1,0:T(1,128)S(1)}, f32[24,1,1024]{2,1,0:T(1,128)S(1)}, u32[]{:S(2)}, u32[]{:S(2)}) collective-permute-start(f32[24,1,1024]{2,1,0:T(1,128)S(1)} %get-tuple-element.108), channel_id=1, source_target_pairs={{0,1},{1,2},{2,3},{4,5},{5,6},{6,7},{8,9},{9,10},{10,11},{12,13},{... | collective-permute-start | bytes 294920 | tf_op jit(solution)/shard_map/ppermute | solution.py:30
  312.7 3.1 collective-permute-start.33
  315.9 6.5 %collective-permute-start.34 = (f32[24,1,1024]{2,1,0:T(1,128)S(1)}, f32[24,1,1024]{2,1,0:T(1,128)S(1)}, u32[]{:S(2)}, u32[]{:S(2)}) collective-permute-start(f32[24,1,1024]{2,1,0:T(1,128)S(1)} %get-tuple-element.105), channel_id=1, source_target_pairs={{1,0},{2,1},{3,2},{5,4},{6,5},{7,6},{9,8},{10,9},{11,10},{13,12},{... | collective-permute-start | bytes 294920 | tf_op jit(solution)/shard_map/ppermute | solution.py:33
  317.2 6.8 %collective-permute-start.35 = (f32[24,1,1024]{2,1,0:T(1,128)S(1)}, f32[24,1,1024]{2,1,0:T(1,128)S(1)}, u32[]{:S(2)}, u32[]{:S(2)}) collective-permute-start(f32[24,1,1024]{2,1,0:T(1,128)S(1)} %get-tuple-element.106), channel_id=1, source_target_pairs={{0,1},{1,2},{2,3},{4,5},{5,6},{6,7},{8,9},{9,10},{10,11},{12,13},{... | collective-permute-start | bytes 294920 | tf_op jit(solution)/shard_map/ppermute | solution.py:30
  327.1 6.0 collective-permute-start.36
  333.3 6.9 %collective-permute-start.37 = (f32[24,1,1024]{2,1,0:T(1,128)S(1)}, f32[24,1,1024]{2,1,0:T(1,128)S(1)}, u32[]{:S(2)}, u32[]{:S(2)}) collective-permute-start(f32[24,1,1024]{2,1,0:T(1,128)S(1)} %get-tuple-element.103), channel_id=1, source_target_pairs={{1,0},{2,1},{3,2},{5,4},{6,5},{7,6},{9,8},{10,9},{11,10},{13,12},{... | collective-permute-start | bytes 294920 | tf_op jit(solution)/shard_map/ppermute | solution.py:33
  334.7 7.2 %collective-permute-start.38 = (f32[24,1,1024]{2,1,0:T(1,128)S(1)}, f32[24,1,1024]{2,1,0:T(1,128)S(1)}, u32[]{:S(2)}, u32[]{:S(2)}) collective-permute-start(f32[24,1,1024]{2,1,0:T(1,128)S(1)} %get-tuple-element.104), channel_id=1, source_target_pairs={{0,1},{1,2},{2,3},{4,5},{5,6},{6,7},{8,9},{9,10},{10,11},{12,13},{... | collective-permute-start | bytes 294920 | tf_op jit(solution)/shard_map/ppermute | solution.py:30
  368.2 3.1 collective-permute-start.39
  371.4 6.5 %collective-permute-start.40 = (f32[24,1,1024]{2,1,0:T(1,128)S(1)}, f32[24,1,1024]{2,1,0:T(1,128)S(1)}, u32[]{:S(2)}, u32[]{:S(2)}) collective-permute-start(f32[24,1,1024]{2,1,0:T(1,128)S(1)} %get-tuple-element.101), channel_id=1, source_target_pairs={{1,0},{2,1},{3,2},{5,4},{6,5},{7,6},{9,8},{10,9},{11,10},{13,12},{... | collective-permute-start | bytes 294920 | tf_op jit(solution)/shard_map/ppermute | solution.py:33
  372.7 6.8 %collective-permute-start.41 = (f32[24,1,1024]{2,1,0:T(1,128)S(1)}, f32[24,1,1024]{2,1,0:T(1,128)S(1)}, u32[]{:S(2)}, u32[]{:S(2)}) collective-permute-start(f32[24,1,1024]{2,1,0:T(1,128)S(1)} %get-tuple-element.102), channel_id=1, source_target_pairs={{0,1},{1,2},{2,3},{4,5},{5,6},{6,7},{8,9},{9,10},{10,11},{12,13},{... | collective-permute-start | bytes 294920 | tf_op jit(solution)/shard_map/ppermute | solution.py:30
  382.6 6.0 collective-permute-start.42
  388.7 6.9 %collective-permute-start.43 = (f32[24,1,1024]{2,1,0:T(1,128)S(1)}, f32[24,1,1024]{2,1,0:T(1,128)S(1)}, u32[]{:S(2)}, u32[]{:S(2)}) collective-permute-start(f32[24,1,1024]{2,1,0:T(1,128)S(1)} %get-tuple-element.99), channel_id=1, source_target_pairs={{1,0},{2,1},{3,2},{5,4},{6,5},{7,6},{9,8},{10,9},{11,10},{13,12},{... | collective-permute-start | bytes 294920 | tf_op jit(solution)/shard_map/ppermute | solution.py:33
  390.2 7.2 %collective-permute-start.44 = (f32[24,1,1024]{2,1,0:T(1,128)S(1)}, f32[24,1,1024]{2,1,0:T(1,128)S(1)}, u32[]{:S(2)}, u32[]{:S(2)}) collective-permute-start(f32[24,1,1024]{2,1,0:T(1,128)S(1)} %get-tuple-element.100), channel_id=1, source_target_pairs={{0,1},{1,2},{2,3},{4,5},{5,6},{6,7},{8,9},{9,10},{10,11},{12,13},{... | collective-permute-start | bytes 294920 | tf_op jit(solution)/shard_map/ppermute | solution.py:30
  401.0 22.2 %copy-start.10 = (f32[24,8,1024]{2,1,0:T(8,128)S(1)}, f32[24,8,1024]{2,1,0:T(8,128)}, u32[]{:S(2)}) copy-start(f32[24,8,1024]{2,1,0:T(8,128)} %copy-done.9) | copy-start | bytes 2359300
  424.2 3.1 collective-permute-start.45
  427.5 6.5 %collective-permute-start.46 = (f32[24,1,1024]{2,1,0:T(1,128)S(1)}, f32[24,1,1024]{2,1,0:T(1,128)S(1)}, u32[]{:S(2)}, u32[]{:S(2)}) collective-permute-start(f32[24,1,1024]{2,1,0:T(1,128)S(1)} %get-tuple-element.97), channel_id=1, source_target_pairs={{1,0},{2,1},{3,2},{5,4},{6,5},{7,6},{9,8},{10,9},{11,10},{13,12},{... | collective-permute-start | bytes 294920 | tf_op jit(solution)/shard_map/ppermute | solution.py:33
  428.8 6.8 %collective-permute-start.47 = (f32[24,1,1024]{2,1,0:T(1,128)S(1)}, f32[24,1,1024]{2,1,0:T(1,128)S(1)}, u32[]{:S(2)}, u32[]{:S(2)}) collective-permute-start(f32[24,1,1024]{2,1,0:T(1,128)S(1)} %get-tuple-element.98), channel_id=1, source_target_pairs={{0,1},{1,2},{2,3},{4,5},{5,6},{6,7},{8,9},{9,10},{10,11},{12,13},{... | collective-permute-start | bytes 294920 | tf_op jit(solution)/shard_map/ppermute | solution.py:30
  439.2 7.0 %collective-permute-start.48 = (f32[8,1024]{1,0:T(8,128)S(1)}, f32[8,1024]{1,0:T(8,128)S(1)}, u32[]{:S(2)}, u32[]{:S(2)}) collective-permute-start(f32[8,1024]{1,0:T(8,128)S(1)} %slice_bitcast_fusion.1), channel_id=1, source_target_pairs={{0,4},{4,8},{8,12},{12,16},{16,20},{20,24},{24,28},{28,32},{32,36}... | collective-permute-start | bytes 98312 | tf_op jit(solution)/shard_map/ppermute | solution.py:22
  446.3 7.1 %collective-permute-start.49 = (f32[24,1,1024]{2,1,0:T(1,128)S(1)}, f32[24,1,1024]{2,1,0:T(1,128)S(1)}, u32[]{:S(2)}, u32[]{:S(2)}) collective-permute-start(f32[24,1,1024]{2,1,0:T(1,128)S(1)} %get-tuple-element.94), channel_id=1, source_target_pairs={{1,0},{2,1},{3,2},{5,4},{6,5},{7,6},{9,8},{10,9},{11,10},{13,12},{... | collective-permute-start | bytes 294920 | tf_op jit(solution)/shard_map/ppermute | solution.py:33
  447.9 7.3 %collective-permute-start.50 = (f32[24,1,1024]{2,1,0:T(1,128)S(1)}, f32[24,1,1024]{2,1,0:T(1,128)S(1)}, u32[]{:S(2)}, u32[]{:S(2)}) collective-permute-start(f32[24,1,1024]{2,1,0:T(1,128)S(1)} %get-tuple-element.95), channel_id=1, source_target_pairs={{0,1},{1,2},{2,3},{4,5},{5,6},{6,7},{8,9},{9,10},{10,11},{12,13},{... | collective-permute-start | bytes 294920 | tf_op jit(solution)/shard_map/ppermute | solution.py:30
  480.9 3.2 collective-permute-start.51
  484.9 6.5 %collective-permute-start.52 = (f32[24,1,1024]{2,1,0:T(1,128)S(1)}, f32[24,1,1024]{2,1,0:T(1,128)S(1)}, u32[]{:S(2)}, u32[]{:S(2)}) collective-permute-start(f32[24,1,1024]{2,1,0:T(1,128)S(1)} %get-tuple-element.92), channel_id=1, source_target_pairs={{1,0},{2,1},{3,2},{5,4},{6,5},{7,6},{9,8},{10,9},{11,10},{13,12},{... | collective-permute-start | bytes 294920 | tf_op jit(solution)/shard_map/ppermute | solution.py:33
  486.2 6.8 %collective-permute-start.53 = (f32[24,1,1024]{2,1,0:T(1,128)S(1)}, f32[24,1,1024]{2,1,0:T(1,128)S(1)}, u32[]{:S(2)}, u32[]{:S(2)}) collective-permute-start(f32[24,1,1024]{2,1,0:T(1,128)S(1)} %get-tuple-element.93), channel_id=1, source_target_pairs={{0,1},{1,2},{2,3},{4,5},{5,6},{6,7},{8,9},{9,10},{10,11},{12,13},{... | collective-permute-start | bytes 294920 | tf_op jit(solution)/shard_map/ppermute | solution.py:30
  497.1 7.2 %collective-permute-start.54 = (f32[8,1024]{1,0:T(8,128)S(1)}, f32[8,1024]{1,0:T(8,128)S(1)}, u32[]{:S(2)}, u32[]{:S(2)}) collective-permute-start(f32[8,1024]{1,0:T(8,128)S(1)} %slice_bitcast_fusion), channel_id=1, source_target_pairs={{0,4},{4,8},{8,12},{12,16},{16,20},{20,24},{24,28},{28,32},{32,36}... | collective-permute-start | bytes 98312 | tf_op jit(solution)/shard_map/ppermute | solution.py:22
  504.4 6.7 %collective-permute-start.55 = (f32[24,1,1024]{2,0,1:T(8,128)S(1)}, f32[24,1,1024]{2,0,1:T(8,128)S(1)}, u32[]{:S(2)}, u32[]{:S(2)}) collective-permute-start(f32[24,1,1024]{2,0,1:T(8,128)S(1)} %get-tuple-element.89), channel_id=1, source_target_pairs={{1,0},{2,1},{3,2},{5,4},{6,5},{7,6},{9,8},{10,9},{11,10},{13,12},{... | collective-permute-start | bytes 294920 | tf_op jit(solution)/shard_map/ppermute | solution.py:33
  505.7 7.2 %collective-permute-start.56 = (f32[24,1,1024]{2,0,1:T(8,128)S(1)}, f32[24,1,1024]{2,0,1:T(8,128)S(1)}, u32[]{:S(2)}, u32[]{:S(2)}) collective-permute-start(f32[24,1,1024]{2,0,1:T(8,128)S(1)} %get-tuple-element.90), channel_id=1, source_target_pairs={{0,1},{1,2},{2,3},{4,5},{5,6},{6,7},{8,9},{9,10},{10,11},{12,13},{... | collective-permute-start | bytes 294920 | tf_op jit(solution)/shard_map/ppermute | solution.py:30
  539.8 8.5 %collective-permute-start.57 = (f32[8,1024]{1,0:T(8,128)S(1)}, f32[8,1024]{1,0:T(8,128)S(1)}, u32[]{:S(2)}, u32[]{:S(2)}) collective-permute-start(f32[8,1024]{1,0:T(8,128)S(1)} %bitcast.223), channel_id=1, source_target_pairs={{4,0},{8,4},{12,8},{16,12},{20,16},{24,20},{28,24},{32,28},{36,32}... | collective-permute-start | bytes 98312 | tf_op jit(solution)/shard_map/ppermute | solution.py:22
  549.5 7.4 %collective-permute-start.58 = (f32[24,1,1024]{2,0,1:T(8,128)S(1)}, f32[24,1,1024]{2,0,1:T(8,128)S(1)}, u32[]{:S(2)}, u32[]{:S(2)}) collective-permute-start(f32[24,1,1024]{2,0,1:T(8,128)S(1)} %get-tuple-element.87), channel_id=1, source_target_pairs={{1,0},{2,1},{3,2},{5,4},{6,5},{7,6},{9,8},{10,9},{11,10},{13,12},{... | collective-permute-start | bytes 294920 | tf_op jit(solution)/shard_map/ppermute | solution.py:33
  550.8 7.6 %collective-permute-start.59 = (f32[24,1,1024]{2,0,1:T(8,128)S(1)}, f32[24,1,1024]{2,0,1:T(8,128)S(1)}, u32[]{:S(2)}, u32[]{:S(2)}) collective-permute-start(f32[24,1,1024]{2,0,1:T(8,128)S(1)} %get-tuple-element.88), channel_id=1, source_target_pairs={{0,1},{1,2},{2,3},{4,5},{5,6},{6,7},{8,9},{9,10},{10,11},{12,13},{... | collective-permute-start | bytes 294920 | tf_op jit(solution)/shard_map/ppermute | solution.py:30
  (69 other events, 942.0 us)
where the time goes:
time: 631 us; the launch traced here: 619 us
  starting transfers between devices  186 us (29%)
  blocking collectives  159 us (25%)
  matrix products  94.8 us (15%)
  other arithmetic  87.8 us (14%)
  waiting for transfers between devices  69.2 us (11%)
  local copies, waits for them, and re-layouts  13.4 us (2%)
  between operations  9.15 us (1%)
    all_to_all x9, blocking collectives, copy_for_each(): return lax.all_to_all(copies, axis, split_axis=0, concat_axis=0, tiled=True)  114 us
    ppermute x20, starting transfers between devices, with_halo(): lax.ppermute(lax.slice_in_dim(block, block.shape[dim] - width, None, axis...  92.2 us
    ppermute x20, starting transfers between devices, passed_along(): lax.ppermute(value, axis, [(source, source + steps) for source in range(l...  60 us
    dot_general x10, matrix products, apply_rows(): lax.dot_general(inputs_low, matrix, (((1,), (1,)), ((), ())), preferred_e...  58 us
    psum x4, blocking collectives, by_axis(): x = lax.psum(x, axis)  45.6 us
    ppermute x20, waiting for transfers between devices, with_halo(): lax.ppermute(lax.slice_in_dim(block, block.shape[dim] - width, None, axis...  32.6 us
    ppermute x20, starting transfers between devices, with_halo(): lax.ppermute(lax.slice_in_dim(block, 0, width, axis=dim), axis, backward)  27 us
    reduce_sum x10, other arithmetic, local(): primal_square = jnp.sum(primal * primal)  26.9 us
  transfers between devices with their start and end apart: 61, of which 58 were waited for; matrix products, arithmetic and copies ran while one was open for 2% of the time, Pallas kernels for 0%

commit v1 on v0

v1 whole, which is shorter than its diff:
```python
import functools

import jax
import jax.numpy as jnp
from jax import lax
from jax.experimental import pallas as pl
from jax.experimental.pallas import tpu as pltpu
from jax.sharding import PartitionSpec as P

GX = 32
GY = 32
GZ = 32
ITERS = 10
PLANES = 8
CHUNKS = 8
ROWS = 24
LANES = 128
WIDTH = 512
PLANE = 1024
diffusion = 0.15
epsilon = 1e-06
MESH = pl.DeviceIdType.MESH
F32 = jnp.float32
BF16 = jnp.bfloat16


def in_plane(chunks, across):
    lane = lax.broadcasted_iota(jnp.int32, (1, LANES), 1)
    along = lane % GZ
    down = [pltpu.roll(c, GZ, 1) for c in chunks]
    up = [pltpu.roll(c, LANES - GZ, 1) for c in chunks]
    out = []
    for j, c in enumerate(chunks):
        below = down[j - 1] if j > 0 else 0.0
        above = up[j + 1] if j < CHUNKS - 1 else 0.0
        y_sum = jnp.where(lane < GZ, below, down[j]) + jnp.where(lane >= LANES - GZ, above, up[j])
        lower = jnp.where(along > 0, pltpu.roll(c, 1, 1), 0.0)
        upper = jnp.where(along < GZ - 1, pltpu.roll(c, LANES - 1, 1), 0.0)
        total = y_sum + lower + upper
        if across is not None:
            total = total + across[j]
        out.append((1.0 - 6.0 * diffusion) * c + diffusion * total)
    return out


def kernel(sections, groups, init_ref, ref_hbm, weight_hbm, matrix_hbm, kkt_ref, bound_ref,
           states_out, boxed_out, dual_out, hist_out,
           ref_ref, weight_ref, mat, mat_t, S, AS, T, D, dual, wref, recip, lhs, halo,
           send24, send0, own24, low24, high24, own0, low0, high0,
           part, part_in, tile, tile_prev, tile_next, k_high, k_low, pul, boxed, scaled,
           hist, first_in, second, second_in,
           load_sem, flat_sem, halo_send, halo_recv, send_sem, recv_sem, hist_send, hist_recv):
    s = lax.axis_index("section")
    x = lax.axis_index("state")
    columns = sections // 2

    def inside(ds, dx):
        return (s + ds >= 0) & (s + ds < sections) & (x + dx >= 0) & (x + dx < groups)

    def rotated(d):
        return lax.rem(x + d, groups)

    pair_count = 2 * groups

    def pair_peer(e):
        flat = lax.rem(lax.rem(s, 2) * groups + x + e, pair_count)
        return (s - lax.rem(s, 2) + flat // groups, lax.rem(flat, groups))

    def column_peer(e):
        return (lax.rem(s // 2 + e, columns) * 2 + lax.rem(s, 2), x)

    zeros = lambda ref: ref.__setitem__(Ellipsis, jnp.zeros(ref.shape, ref.dtype))
    for ref in (halo, own24, low24, high24, own0, low0, high0):
        zeros(ref)

    barrier = pltpu.get_barrier_semaphore()

    def greet(target):
        pl.semaphore_signal(barrier, inc=1, device_id=target, device_id_type=MESH)

    for d in range(1, groups):
        greet((s, rotated(d)))
    for d in range(groups):
        @pl.when(s > 0)
        def _():
            greet((s - 1, rotated(d)))

        @pl.when(s < sections - 1)
        def _():
            greet((s + 1, rotated(d)))
    for e in range(1, columns):
        greet(column_peer(e))

    loads = [pltpu.make_async_copy(matrix_hbm.at[p], mat.at[p + 1], load_sem.at[p]) for p in range(PLANES)]
    flat_loads = []
    for j in range(CHUNKS):
        cells = pl.ds(j * LANES, LANES)
        flat_loads.append(pltpu.make_async_copy(weight_hbm.at[:, cells], weight_ref.at[j], flat_sem.at[0, j]))
        flat_loads.append(pltpu.make_async_copy(ref_hbm.at[:, cells], ref_ref.at[j], flat_sem.at[1, j]))
    for copy in flat_loads + loads:
        copy.start()

    for ref in (AS, T, D, dual, S, boxed, scaled, hist):
        zeros(ref)

    @pl.when(x == 0)
    def _():
        mat[0] = jnp.zeros((PLANE, WIDTH), BF16)

    @pl.when(x == groups - 1)
    def _():
        mat[PLANES + 1] = jnp.zeros((PLANE, WIDTH), BF16)

    neighbours = (
        (s > 0).astype(jnp.int32) * groups
        + (s < sections - 1).astype(jnp.int32) * groups
        + (groups - 1)
        + (columns - 1)
    )
    pl.semaphore_wait(barrier, neighbours)

    def plane_copy(side):
        source = 0 if side == 0 else PLANES - 1
        target = PLANES + 1 if side == 0 else 0
        return pltpu.make_async_remote_copy(
            src_ref=matrix_hbm.at[source], dst_ref=mat.at[target],
            send_sem=halo_send.at[side], recv_sem=halo_recv.at[side],
            device_id=(s, x - 1 if side == 0 else x + 1), device_id_type=MESH)

    @pl.when(x > 0)
    def _():
        plane_copy(0).start()

    @pl.when(x < groups - 1)
    def _():
        plane_copy(1).start()

    kkt = kkt_ref[...]
    high = kkt.astype(BF16)
    k_high[...] = high
    k_low[...] = (kkt - high.astype(F32)).astype(BF16)

    for copy in flat_loads:
        copy.wait()
    for p in range(PLANES):
        for j in range(CHUNKS):
            weight = weight_ref[j, pl.ds(p, ROWS, stride=PLANES), :]
            wref[p, j] = weight * ref_ref[j, pl.ds(p, ROWS, stride=PLANES), :]
            recip[p, j] = 1.0 / (weight + 2.0)

    @pl.when(s == 0)
    def _():
        for p in range(PLANES):
            own = [init_ref[p:p + 1, j * LANES:(j + 1) * LANES] for j in range(CHUNKS)]
            across = []
            for j in range(CHUNKS):
                cells = slice(j * LANES, (j + 1) * LANES)
                total = jnp.zeros((1, LANES), F32)
                if p > 0:
                    total = total + init_ref[p - 1:p, cells]
                if p < PLANES - 1:
                    total = total + init_ref[p + 1:p + 2, cells]
                across.append(total)
            moved = in_plane(own, across)
            for j in range(CHUNKS):
                AS[p, j, 7:8, :] = moved[j]
                if p in (0, PLANES - 1):
                    S[p + 1, j, 7:8, :] = own[j]

    for copy in loads:
        copy.wait()

    @pl.when(x < groups - 1)
    def _():
        plane_copy(0).wait_recv()

    @pl.when(x > 0)
    def _():
        plane_copy(1).wait_recv()

    @pl.when(x > 0)
    def _():
        plane_copy(0).wait_send()

    @pl.when(x < groups - 1)
    def _():
        plane_copy(1).wait_send()

    def turn(p, carry):
        mat_t[p] = mat[p].T
        return carry

    lax.fori_loop(0, PLANES + 2, turn, 0)

    penalty = float(GX * GY * GZ) / WIDTH
    not_last = jnp.where(s < sections - 1, 1.0, 0.0).astype(F32)
    cross = [(0, -1), (0, 1), (1, 0), (1, 1), (1, -1), (-1, 0), (-1, 1), (-1, -1)]
    base_index = len(cross)

    def messages(slot):
        side = 2 * PLANE
        sources = [
            (lhs.at[:, pl.ds(0, side)], halo.at[slot, 1]),
            (lhs.at[:, pl.ds(PLANES * PLANE, side)], halo.at[slot, 0]),
            (send24.at[pl.ds(1, PLANES)], own24.at[slot]),
            (send24.at[PLANES + 1], low24.at[slot]),
            (send24.at[0], high24.at[slot]),
            (send0, own0.at[slot]),
            (send0.at[PLANES - 1], low0.at[slot]),
            (send0.at[0], high0.at[slot]),
        ]
        return sources

    def cross_copy(i, slot):
        ds, dx = cross[i]
        source, target = messages(slot)[i]
        return pltpu.make_async_remote_copy(
            src_ref=source, dst_ref=target, send_sem=send_sem.at[i], recv_sem=recv_sem.at[slot, i],
            device_id=(s + ds, x + dx), device_id_type=MESH)

    def peer_copy(d, slot):
        i = base_index + d - 1
        return pltpu.make_async_remote_copy(
            src_ref=part, dst_ref=part_in.at[slot, d - 1], send_sem=send_sem.at[i],
            recv_sem=recv_sem.at[slot, i], device_id=(s, rotated(d)), device_id_type=MESH)

    def tile_copy(ds, d, slot):
        i = base_index + groups - 1 + (groups if ds > 0 else 0) + d
        target = tile_prev if ds > 0 else tile_next
        return pltpu.make_async_remote_copy(
            src_ref=tile, dst_ref=target.at[slot, d], send_sem=send_sem.at[i],
            recv_sem=recv_sem.at[slot, i], device_id=(s + ds, rotated(d)), device_id_type=MESH)

    def iteration(k, carry):
        slot = lax.rem(k, 2)

        def apply(p, c):
            chunks = [S[p + 1, j, 8:32, :] for j in range(CHUNKS)]
            across = [S[p, j, 8:32, :] + S[p + 2, j, 8:32, :] for j in range(CHUNKS)]
            for j, value in enumerate(in_plane(chunks, across)):
                AS[p, j, 8:32, :] = value
            for j in range(CHUNKS):
                moved = AS[p, j, pl.ds(7, ROWS), :]
                tail = -AS[p, j, pl.ds(31, 8), :]
                body = chunks[j] + dual[p, j] - moved
                T[p + 1, j, 0:24, :] = body
                T[p + 1, j, 24:32, :] = tail
                full = jnp.concatenate([body, tail], 0)
                lhs[:, pl.ds(pl.multiple_of((p + 1) * PLANE, PLANE) + j * LANES, LANES)] = full.astype(BF16)
                send24[p + 1, j:j + 1, :] = tail[0:1]
                send0[p, j:j + 1, :] = body[0:1]
            return c

        lax.fori_loop(0, PLANES, apply, 0)
        for p, q in ((0, 1), (PLANES + 1, PLANES)):
            for j in range(CHUNKS):
                full = -diffusion * S[q, j, pl.ds(7, 32), :]
                T[p, j] = full
                lhs[:, pl.ds(p * PLANE + j * LANES, LANES)] = full.astype(BF16)
                send24[p, j:j + 1, :] = full[24:25]

        for i, (ds, dx) in enumerate(cross):
            @pl.when(inside(ds, dx))
            def _():
                cross_copy(i, slot).start()

        part[...] = jnp.dot(lhs[...], mat[...].reshape((PLANES + 2) * PLANE, WIDTH), preferred_element_type=F32)
        for c in range(4):
            cells = slice(c * LANES, (c + 1) * LANES)
            tile[c:c + 1, :] = part[0:1, cells]
            tile[c + 4:c + 5, :] = part[24:25, cells]
        for d in range(1, groups):
            peer_copy(d, slot).start()
        for d in range(groups):
            @pl.when(s < sections - 1)
            def _():
                tile_copy(1, d, slot).start()

            @pl.when(s > 0)
            def _():
                tile_copy(-1, d, slot).start()

        for i, (ds, dx) in enumerate(cross):
            @pl.when(inside(-ds, -dx))
            def _():
                cross_copy(i, slot).wait_recv()

        for j in range(CHUNKS):
            low = slice(j * LANES, (j + 1) * LANES)
            high_ = slice(PLANE + j * LANES, PLANE + (j + 1) * LANES)
            T[1, j] = T[1, j] + halo[slot, 0, :, high_].astype(F32)
            T[PLANES, j] = T[PLANES, j] + halo[slot, 1, :, low].astype(F32)
            T[0, j] = T[0, j] + halo[slot, 0, :, low].astype(F32)
            T[PLANES + 1, j] = T[PLANES + 1, j] + halo[slot, 1, :, high_].astype(F32)
            T[0, j, 24:25, :] += low0[slot, j:j + 1, :]
            T[PLANES + 1, j, 24:25, :] += high0[slot, j:j + 1, :]
            T[1, j, 0:1, :] += low24[slot, j:j + 1, :]
            T[PLANES, j, 0:1, :] += high24[slot, j:j + 1, :]

        def complete(p, c):
            for j in range(CHUNKS):
                T[p + 1, j, 0:1, :] += own24[slot, p, j:j + 1, :]
                T[p + 1, j, 24:25, :] += own0[slot, p, j:j + 1, :]
            return c

        lax.fori_loop(0, PLANES, complete, 0)

        for d in range(1, groups):
            peer_copy(d, slot).wait_recv()
        for d in range(groups):
            @pl.when(s > 0)
            def _():
                tile_copy(1, d, slot).wait_recv()

            @pl.when(s < sections - 1)
            def _():
                tile_copy(-1, d, slot).wait_recv()

        total = part[...]
        for d in range(1, groups):
            total = total + part_in[slot, d - 1]
        pul[...] = total + penalty * (boxed[...] - scaled[...])

        @pl.when(s > 0)
        def _():
            incoming = tile_prev[slot, 0]
            for d in range(1, groups):
                incoming = incoming + tile_prev[slot, d]
            for c in range(4):
                cells = slice(c * LANES, (c + 1) * LANES)
                pul[0:1, cells] += incoming[c + 4:c + 5]

        @pl.when(s < sections - 1)
        def _():
            incoming = tile_next[slot, 0]
            for d in range(1, groups):
                incoming = incoming + tile_next[slot, d]
            for c in range(4):
                cells = slice(c * LANES, (c + 1) * LANES)
                pul[24:25, cells] += incoming[c:c + 1]

        rhs = pul[...]
        rhs_high = rhs.astype(BF16)
        rhs_low = (rhs - rhs_high.astype(F32)).astype(BF16)
        stacked = jnp.dot(jnp.concatenate([rhs_high, rhs_low], 0), k_high[...], preferred_element_type=F32)
        inputs = stacked[0:32] + stacked[32:64] + jnp.dot(rhs_high, k_low[...], preferred_element_type=F32)
        bound = bound_ref[...]
        boxed_new = jnp.clip(inputs + scaled[...], -bound, bound)
        gap = inputs - boxed_new
        scaled[...] = scaled[...] + gap
        boxed[...] = boxed_new
        inputs_low = inputs.astype(BF16)
        gap_sum = jnp.sum(gap[0:ROWS] * gap[0:ROWS], axis=(0, 1), keepdims=True)

        def drive(p, c):
            driven = jnp.dot(inputs_low, mat_t[p], preferred_element_type=F32)
            for j in range(CHUNKS):
                piece = driven[:, j * LANES:(j + 1) * LANES]
                D[p, j, 0:24, :] = T[p, j, 0:24, :] - piece[0:24]
                D[p, j, 24:32, :] = (T[p, j, 24:32, :] - piece[24:32]) * not_last
            return c

        lax.fori_loop(1, PLANES + 1, drive, 0)

        @pl.when(x > 0)
        def _():
            drive(0, 0)

        @pl.when(x < groups - 1)
        def _():
            drive(PLANES + 1, 0)

        def update(p, acc):
            chunks = [D[p + 1, j, pl.ds(1, ROWS), :] for j in range(CHUNKS)]
            across = [D[p, j, pl.ds(1, ROWS), :] + D[p + 2, j, pl.ds(1, ROWS), :] for j in range(CHUNKS)]
            back = in_plane(chunks, across)
            for j in range(CHUNKS):
                old = S[p + 1, j, 8:32, :]
                defect = D[p + 1, j, 0:24, :]
                fresh = (wref[p, j] + (2.0 * old - defect) + back[j]) * recip[p, j]
                old_dual = dual[p, j]
                new_dual = fresh - old + defect
                primal = new_dual - old_dual
                S[p + 1, j, 8:32, :] = fresh
                dual[p, j] = new_dual
                square = primal * primal
                acc = acc + (square[0:8] + square[8:16] + square[16:24])
            return acc

        acc = lax.fori_loop(0, PLANES, update, jnp.zeros((8, LANES), F32))
        primal_sum = jnp.sum(acc, axis=(0, 1), keepdims=True)
        row = lax.broadcasted_iota(jnp.int32, (8, LANES), 0)
        column = lax.broadcasted_iota(jnp.int32, (8, LANES), 1)
        hist[...] += jnp.where((column == k) & (row == 0), primal_sum, 0.0) + jnp.where(
            (column == k) & (row == 1), gap_sum, 0.0)

        for i, (ds, dx) in enumerate(cross):
            @pl.when(inside(ds, dx))
            def _():
                cross_copy(i, slot).wait_send()
        for d in range(1, groups):
            peer_copy(d, slot).wait_send()
        for d in range(groups):
            @pl.when(s < sections - 1)
            def _():
                tile_copy(1, d, slot).wait_send()

            @pl.when(s > 0)
            def _():
                tile_copy(-1, d, slot).wait_send()
        return carry

    lax.fori_loop(0, ITERS, iteration, 0)

    def first_copy(e):
        return pltpu.make_async_remote_copy(
            src_ref=hist, dst_ref=first_in.at[e - 1], send_sem=hist_send.at[e - 1], recv_sem=hist_recv.at[e - 1],
            device_id=pair_peer(e), device_id_type=MESH)

    def second_copy(e):
        i = pair_count - 2 + e
        return pltpu.make_async_remote_copy(
            src_ref=second, dst_ref=second_in.at[e - 1], send_sem=hist_send.at[i], recv_sem=hist_recv.at[i],
            device_id=column_peer(e), device_id_type=MESH)

    for e in range(1, pair_count):
        first_copy(e).start()

    for p in range(PLANES):
        for j in range(CHUNKS):
            ref_ref[j, pl.ds(p, ROWS, stride=PLANES), :] = S[p + 1, j, 8:32, :]
            weight_ref[j, pl.ds(p, ROWS, stride=PLANES), :] = dual[p, j]
    stores = []
    for j in range(CHUNKS):
        cells = pl.ds(j * LANES, LANES)
        stores.append(pltpu.make_async_copy(ref_ref.at[j], states_out.at[:, cells], flat_sem.at[0, j]))
        stores.append(pltpu.make_async_copy(weight_ref.at[j], dual_out.at[:, cells], flat_sem.at[1, j]))
    for copy in stores:
        copy.start()
    boxed_out[...] = boxed[0:ROWS]

    for e in range(1, pair_count):
        first_copy(e).wait()
    total = hist[...]
    for e in range(1, pair_count):
        total = total + first_in[e - 1]
    second[...] = total
    for e in range(1, columns):
        second_copy(e).start()
    for e in range(1, columns):
        second_copy(e).wait()
    for e in range(1, columns):
        total = total + second_in[e - 1]
    row = lax.broadcasted_iota(jnp.int32, (8, LANES), 0)
    cells = float(ROWS * sections * GX * GY * GZ)
    inputs_count = float(ROWS * sections * WIDTH * groups)
    for copy in stores:
        copy.wait()
    hist_out[...] = jnp.sqrt(jnp.where(row == 0, total * (1.0 / cells), total * (1.0 / inputs_count)) + epsilon)


def solution(mesh):
    sections, groups = mesh.shape["section"], mesh.shape["state"]
    columns = sections // 2

    def local(initial_state, state_ref, state_weight, input_matrix, kkt_inverse, input_bound):
        vmem = pl.BlockSpec(memory_space=pltpu.VMEM)
        any_space = pl.BlockSpec(memory_space=pl.ANY)
        flat = (ROWS * PLANES, PLANE)
        V = pltpu.VMEM
        DMA = pltpu.SemaphoreType.DMA
        message_count = 8 + groups - 1 + 2 * groups
        compact = (CHUNKS, LANES)
        states, boxed, dual_vars, record = pl.pallas_call(
            functools.partial(kernel, sections, groups),
            out_shape=(
                jax.ShapeDtypeStruct(flat, F32),
                jax.ShapeDtypeStruct((ROWS, WIDTH), F32),
                jax.ShapeDtypeStruct(flat, F32),
                jax.ShapeDtypeStruct((8, LANES), F32),
            ),
            in_specs=[vmem, any_space, any_space, any_space, vmem, vmem],
            out_specs=(any_space, vmem, any_space, vmem),
            scratch_shapes=[
                V((CHUNKS, ROWS * PLANES, LANES), F32),
                V((CHUNKS, ROWS * PLANES, LANES), F32),
                V((PLANES + 2, PLANE, WIDTH), BF16),
                V((PLANES + 2, WIDTH, PLANE), BF16),
                V((PLANES + 2, CHUNKS, 40, LANES), F32),
                V((PLANES, CHUNKS, 40, LANES), F32),
                V((PLANES + 2, CHUNKS, 32, LANES), F32),
                V((PLANES + 2, CHUNKS, 32, LANES), F32),
                V((PLANES, CHUNKS, ROWS, LANES), F32),
                V((PLANES, CHUNKS, ROWS, LANES), F32),
                V((PLANES, CHUNKS, ROWS, LANES), F32),
                V((32, (PLANES + 2) * PLANE), BF16),
                V((2, 2, 32, 2 * PLANE), BF16),
                V((PLANES + 2, *compact), F32),
                V((PLANES, *compact), F32),
                V((2, PLANES, *compact), F32),
                V((2, *compact), F32),
                V((2, *compact), F32),
                V((2, PLANES, *compact), F32),
                V((2, *compact), F32),
                V((2, *compact), F32),
                V((32, WIDTH), F32),
                V((2, groups - 1, 32, WIDTH), F32),
                V(compact, F32),
                V((2, groups, *compact), F32),
                V((2, groups, *compact), F32),
                V((WIDTH, WIDTH), BF16),
                V((WIDTH, WIDTH), BF16),
                V((32, WIDTH), F32),
                V((32, WIDTH), F32),
                V((32, WIDTH), F32),
                V(compact, F32),
                V((2 * groups - 1, *compact), F32),
                V(compact, F32),
                V((max(columns - 1, 1), *compact), F32),
                DMA((PLANES,)),
                DMA((2, CHUNKS)),
                DMA((2,)),
                DMA((2,)),
                DMA((message_count,)),
                DMA((2, message_count)),
                DMA((2 * groups + columns,)),
                DMA((2 * groups + columns,)),
            ],
            compiler_params=pltpu.CompilerParams(
                collective_id=0, has_side_effects=True, vmem_limit_bytes=64000 * 1024),
        )(
            initial_state,
            state_ref.reshape(flat),
            state_weight.reshape(flat),
            input_matrix,
            kkt_inverse,
            input_bound.reshape(1, WIDTH),
        )
        return (
            states.reshape(state_ref.shape),
            boxed,
            dual_vars.reshape(state_ref.shape),
            record[0:2, 0:ITERS].T,
        )

    return jax.shard_map(
        local,
        mesh=mesh,
        in_specs=(
            P("state", None),
            P("section", "state", None),
            P("section", "state", None),
            P("state", None, None),
            P(),
            P(),
        ),
        out_specs=(P("section", "state", None), P("section", None), P("section", "state", None), P()),
        check_vma=False,
    )
```

time: 631 us -> 212 us (0.34); the launches traced: 619 us -> 212 us
  Pallas kernels: 0 us -> 204 us
  starting transfers between devices: 186 us -> 0 us
  blocking collectives: 159 us -> 0 us
  matrix products: 94.8 us -> 0 us
  other arithmetic: 87.8 us -> 0 us
  waiting for transfers between devices: 69.2 us -> 0 us
  between operations: 9.15 us -> 0.64 us
  local copies, waits for them, and re-layouts: 13.4 us -> 6.83 us
    pallas_call x0 -> x1, Pallas kernels: none -> 204 us  [local(): pl.pallas_call(functools.partial(kernel, sections, groups), out_shape=(ja...]
    ppermute x60 -> x0, starting transfers between devices: 179 us -> none  [the longest x20 92.2 us: with_halo(): lax.ppermute(lax.slice_in_dim(block, block.shape[dim] - width, None, axis...]
    all_to_all x9 -> x0, blocking collectives: 114 us -> none  [copy_for_each(): return lax.all_to_all(copies, axis, split_axis=0, concat_axis=0, tiled=True)]
    dot_general x30 -> x0, matrix products: 94.8 us -> none  [the longest x10 58 us: apply_rows(): lax.dot_general(inputs_low, matrix, (((1,), (1,)), ((), ())), preferred_e...]
    ppermute x60 -> x0, waiting for transfers between devices: 62.7 us -> none  [the longest x20 32.6 us: with_halo(): lax.ppermute(lax.slice_in_dim(block, block.shape[dim] - width, None, axis...]
    psum x4 -> x0, blocking collectives: 45.6 us -> none  [by_axis(): x = lax.psum(x, axis)]
    reduce_sum x20 -> x0, other arithmetic: 40.4 us -> none  [the longest x10 26.9 us: local(): primal_square = jnp.sum(primal * primal)]
    convert_element_type x9 -> x0, other arithmetic: 17.9 us -> none  [local(): target_low = target.astype(jnp.bfloat16).reshape(section_count, -1)]
  transfers between devices with their start and end apart: 61 -> 0, of which waited for: 58 -> 0; matrix products, arithmetic and copies ran while one was open for 2% -> 0% of each run, Pallas kernels for 0% -> 0%
where the time goes in v1:
time: 212 us
  Pallas kernels  204 us (96%)
  local copies, waits for them, and re-layouts  6.83 us (3%)
    pallas_call x1, Pallas kernels, local(): pl.pallas_call(functools.partial(kernel, sections, groups), out_shape=(ja...  204 us
    unnamed x3, local copies, waits for them, and re-layouts  5.6 us

profile of v1, /device:TPU:0, one launch (start us, length us, event | category | flops | bytes accessed | tf_op | source)
XLA Modules:
  0.0 211.9 jit_solution(11301924878439540193)
XLA Ops:
  0.6 204.5 %shard_map.93 = (f32[192,1024]{1,0:T(8,128)}, f32[24,512]{1,0:T(8,128)}, f32[192,1024]{1,0:T(8,128)}, f32[8,128]{1,0:T(8,128)}) custom-call(f32[8,1024]{1,0:T(8,128)} %init_ref.1, f32[192,1024]{1,0:T(8,128)} %bitcast.7, f32[192,1024]{1,0:T(8,128)} %bitcast.8, bf16[8,1024,512]{2,1,0:T(8,128)(2,1)} %matrix_hbm.1, f32[512,512]{1,0:T(8,128)} %kkt_ref.1, ...), custom_call_target="tpu_custom_call" | custom-call | tf_op jit(solution)/shard_map/pallas_call | solution.py:474
  205.1 1.2 slice_bitcast_fusion
  206.3 2.1 copy.13
  208.4 1.4 copy.14
  209.9 2.1 copy.15

commit v2 on v1

v2 whole, which is shorter than its diff:
```python
import functools

import jax
import jax.numpy as jnp
from jax import lax
from jax.experimental import pallas as pl
from jax.experimental.pallas import tpu as pltpu
from jax.sharding import PartitionSpec as P

GX = 32
GY = 32
GZ = 32
ITERS = 10
PIECES = 4
HALO_FIRST = True
PLANES = 8
CHUNKS = 8
ROWS = 24
LANES = 128
WIDTH = 512
PLANE = 1024
diffusion = 0.15
epsilon = 1e-06
MESH = pl.DeviceIdType.MESH
F32 = jnp.float32
BF16 = jnp.bfloat16


def in_plane(chunks, across):
    lane = lax.broadcasted_iota(jnp.int32, (1, LANES), 1)
    along = lane % GZ
    down = [pltpu.roll(c, GZ, 1) for c in chunks]
    up = [pltpu.roll(c, LANES - GZ, 1) for c in chunks]
    out = []
    for j, c in enumerate(chunks):
        below = down[j - 1] if j > 0 else 0.0
        above = up[j + 1] if j < CHUNKS - 1 else 0.0
        y_sum = jnp.where(lane < GZ, below, down[j]) + jnp.where(lane >= LANES - GZ, above, up[j])
        lower = jnp.where(along > 0, pltpu.roll(c, 1, 1), 0.0)
        upper = jnp.where(along < GZ - 1, pltpu.roll(c, LANES - 1, 1), 0.0)
        total = y_sum + lower + upper
        if across is not None:
            total = total + across[j]
        out.append((1.0 - 6.0 * diffusion) * c + diffusion * total)
    return out


def kernel(sections, groups, init_ref, ref_hbm, weight_hbm, matrix_hbm, kkt_ref, bound_ref,
           states_out, boxed_out, dual_out, hist_out,
           ref_ref, weight_ref, mat, mat_t, S, AS, T, D, dual, wref, recip, lhs, halo,
           send24, send0, own24, low24, high24, own0, low0, high0,
           part, part_low, part_in, init_in, tile, tile_prev, tile_next, k_high, k_low, pul, boxed, scaled,
           hist, first_in, second, second_in,
           load_sem, flat_sem, halo_send, halo_recv, pass_send, pass_recv, init_send, init_recv, send_sem, recv_sem, hist_send, hist_recv):
    s = lax.axis_index("section")
    x = lax.axis_index("state")
    columns = sections // 2

    def inside(ds, dx):
        return (s + ds >= 0) & (s + ds < sections) & (x + dx >= 0) & (x + dx < groups)

    def rotated(d):
        return lax.rem(x + d, groups)

    pair_count = 2 * groups

    def pair_peer(e):
        flat = lax.rem(lax.rem(s, 2) * groups + x + e, pair_count)
        return (s - lax.rem(s, 2) + flat // groups, lax.rem(flat, groups))

    def column_peer(e):
        return (lax.rem(s // 2 + e, columns) * 2 + lax.rem(s, 2), x)

    zeros = lambda ref: ref.__setitem__(Ellipsis, jnp.zeros(ref.shape, ref.dtype))
    for ref in (halo, own24, low24, high24, own0, low0, high0, init_in):
        zeros(ref)

    barrier = pltpu.get_barrier_semaphore()

    def greet(target):
        pl.semaphore_signal(barrier, inc=1, device_id=target, device_id_type=MESH)

    for d in range(1, groups):
        greet((s, rotated(d)))
    for d in range(groups):
        @pl.when(s > 0)
        def _():
            greet((s - 1, rotated(d)))

        @pl.when(s < sections - 1)
        def _():
            greet((s + 1, rotated(d)))
    for e in range(1, columns):
        greet(column_peer(e))

    loads = [pltpu.make_async_copy(matrix_hbm.at[p], mat.at[p + 1], load_sem.at[p]) for p in range(PLANES)]
    flat_loads = []
    for j in range(CHUNKS):
        cells = pl.ds(j * LANES, LANES)
        flat_loads.append(pltpu.make_async_copy(weight_hbm.at[:, cells], weight_ref.at[j], flat_sem.at[0, j]))
        flat_loads.append(pltpu.make_async_copy(ref_hbm.at[:, cells], ref_ref.at[j], flat_sem.at[1, j]))
    for copy in flat_loads + loads:
        copy.start()

    for ref in (AS, T, D, dual, S, boxed, scaled, hist):
        zeros(ref)

    @pl.when(x == 0)
    def _():
        mat[0] = jnp.zeros((PLANE, WIDTH), BF16)

    @pl.when(x == groups - 1)
    def _():
        mat[PLANES + 1] = jnp.zeros((PLANE, WIDTH), BF16)

    neighbours = (
        (s > 0).astype(jnp.int32) * groups
        + (s < sections - 1).astype(jnp.int32) * groups
        + (groups - 1)
        + (columns - 1)
    )
    pl.semaphore_wait(barrier, neighbours)

    half = lax.rem(s, 2) * (PLANE // 2)
    twin = s + 1 - 2 * lax.rem(s, 2)
    depth = PLANE // 2 // PIECES

    def plane_copy(side, piece):
        source = 0 if side == 0 else PLANES - 1
        target = PLANES + 1 if side == 0 else 0
        rows = pl.ds(pl.multiple_of(half + piece * depth, depth), depth)
        return pltpu.make_async_remote_copy(
            src_ref=matrix_hbm.at[source, rows], dst_ref=mat.at[target, rows],
            send_sem=halo_send.at[side, piece], recv_sem=halo_recv.at[side, piece],
            device_id=(s, x - 1 if side == 0 else x + 1), device_id_type=MESH)

    def pass_copy(side, piece, start):
        target = PLANES + 1 if side == 0 else 0
        rows = pl.ds(pl.multiple_of(start + piece * depth, depth), depth)
        return pltpu.make_async_remote_copy(
            src_ref=mat.at[target, rows], dst_ref=mat.at[target, rows],
            send_sem=pass_send.at[side, piece], recv_sem=pass_recv.at[side, piece],
            device_id=(twin, x), device_id_type=MESH)

    sends_to = (x > 0, x < groups - 1)
    gets_from = (x < groups - 1, x > 0)

    def init_copy(side):
        return pltpu.make_async_remote_copy(
            src_ref=init_ref, dst_ref=init_in.at[1 - side], send_sem=init_send.at[side],
            recv_sem=init_recv.at[side], device_id=(s, x - 1 if side == 0 else x + 1), device_id_type=MESH)

    for side in range(2):
        @pl.when((s == 0) & sends_to[side])
        def _():
            init_copy(side).start()

        @pl.when(sends_to[side])
        def _():
            for piece in range(PIECES):
                plane_copy(side, piece).start()

    kkt = kkt_ref[...]
    high = kkt.astype(BF16)
    k_high[...] = high
    k_low[...] = (kkt - high.astype(F32)).astype(BF16)

    for copy in flat_loads:
        copy.wait()
    for p in range(PLANES):
        for j in range(CHUNKS):
            weight = weight_ref[j, pl.ds(p, ROWS, stride=PLANES), :]
            wref[p, j] = weight * ref_ref[j, pl.ds(p, ROWS, stride=PLANES), :]
            recip[p, j] = 1.0 / (weight + 2.0)

    penalty = float(GX * GY * GZ) / WIDTH
    not_last = jnp.where(s < sections - 1, 1.0, 0.0).astype(F32)
    has_side = (jnp.where(x > 0, 1.0, 0.0).astype(F32), jnp.where(x < groups - 1, 1.0, 0.0).astype(F32))
    cross = [(0, -1), (0, 1), (1, 0), (1, 1), (1, -1), (-1, 0), (-1, 1), (-1, -1)]
    base_index = len(cross)

    def messages(slot):
        side = 2 * PLANE
        return [
            (lhs.at[:, pl.ds(0, side)], halo.at[slot, 1]),
            (lhs.at[:, pl.ds(PLANES * PLANE, side)], halo.at[slot, 0]),
            (send24.at[pl.ds(1, PLANES)], own24.at[slot]),
            (send24.at[PLANES + 1], low24.at[slot]),
            (send24.at[0], high24.at[slot]),
            (send0, own0.at[slot]),
            (send0.at[PLANES - 1], low0.at[slot]),
            (send0.at[0], high0.at[slot]),
        ]

    def cross_copy(i, slot):
        ds, dx = cross[i]
        source, target = messages(slot)[i]
        return pltpu.make_async_remote_copy(
            src_ref=source, dst_ref=target, send_sem=send_sem.at[i], recv_sem=recv_sem.at[slot, i],
            device_id=(s + ds, x + dx), device_id_type=MESH)

    def peer_copy(d, slot):
        i = base_index + d - 1
        return pltpu.make_async_remote_copy(
            src_ref=part_low, dst_ref=part_in.at[slot, d - 1], send_sem=send_sem.at[i],
            recv_sem=recv_sem.at[slot, i], device_id=(s, rotated(d)), device_id_type=MESH)

    def tile_copy(ds, d, slot):
        i = base_index + groups - 1 + (groups if ds > 0 else 0) + d
        target = tile_prev if ds > 0 else tile_next
        return pltpu.make_async_remote_copy(
            src_ref=tile, dst_ref=target.at[slot, d], send_sem=send_sem.at[i],
            recv_sem=recv_sem.at[slot, i], device_id=(s + ds, rotated(d)), device_id_type=MESH)

    def apply(p):
        chunks = [S[p + 1, j, 8:32, :] for j in range(CHUNKS)]
        across = [S[p, j, 8:32, :] + S[p + 2, j, 8:32, :] for j in range(CHUNKS)]
        for j, value in enumerate(in_plane(chunks, across)):
            AS[p, j, 8:32, :] = value
        for j in range(CHUNKS):
            body = chunks[j] + dual[p, j] - AS[p, j, pl.ds(7, ROWS), :]
            tail = -AS[p, j, pl.ds(31, 8), :]
            T[p + 1, j, 0:24, :] = body
            T[p + 1, j, 24:32, :] = tail
            lhs[:, (p + 1) * PLANE + j * LANES:(p + 1) * PLANE + (j + 1) * LANES] = jnp.concatenate(
                [body, tail], 0).astype(BF16)
            send24[p + 1, j:j + 1, :] = tail[0:1]
            send0[p, j:j + 1, :] = body[0:1]

    def apply_outside(side):
        p, q = ((0, 1), (PLANES + 1, PLANES))[side]
        for j in range(CHUNKS):
            full = (-diffusion * has_side[side]) * S[q, j, pl.ds(7, 32), :]
            T[p, j] = full
            lhs[:, p * PLANE + j * LANES:p * PLANE + (j + 1) * LANES] = full.astype(BF16)
            send24[p, j:j + 1, :] = full[24:25]

    def solve(k, slot):
        total = part[...]
        for d in range(1, groups):
            total = total + part_in[slot, d - 1].astype(F32)
        pul[...] = total + penalty * (boxed[...] - scaled[...])

        @pl.when((s > 0) & (k > 0))
        def _():
            incoming = tile_prev[slot, 0]
            for d in range(1, groups):
                incoming = incoming + tile_prev[slot, d]
            for c in range(4):
                cells = slice(c * LANES, (c + 1) * LANES)
                pul[0:1, cells] += incoming[c + 4:c + 5]

        @pl.when((s < sections - 1) & (k > 0))
        def _():
            incoming = tile_next[slot, 0]
            for d in range(1, groups):
                incoming = incoming + tile_next[slot, d]
            for c in range(4):
                cells = slice(c * LANES, (c + 1) * LANES)
                pul[24:25, cells] += incoming[c:c + 1]

        rhs = pul[...]
        rhs_high = rhs.astype(BF16)
        rhs_low = (rhs - rhs_high.astype(F32)).astype(BF16)
        stacked = jnp.dot(jnp.concatenate([rhs_high, rhs_low], 0), k_high[...], preferred_element_type=F32)
        inputs = stacked[0:32] + stacked[32:64] + jnp.dot(rhs_high, k_low[...], preferred_element_type=F32)
        bound = bound_ref[...]
        boxed_new = jnp.clip(inputs + scaled[...], -bound, bound)
        gap = inputs - boxed_new
        scaled[...] = scaled[...] + gap
        boxed[...] = boxed_new
        gap_sum = jnp.sum(gap[0:ROWS] * gap[0:ROWS], axis=(0, 1), keepdims=True)
        record(k, 1, gap_sum)
        return inputs.astype(BF16)

    def record(k, kind, value):
        row = lax.broadcasted_iota(jnp.int32, (16, LANES), 0)
        column = lax.broadcasted_iota(jnp.int32, (16, LANES), 1)
        hist[...] += jnp.where((column == kind) & (row == k), value, 0.0)

    def drive(p, inputs_low):
        driven = jnp.dot(inputs_low, mat_t[p], preferred_element_type=F32)
        for j in range(CHUNKS):
            piece = driven[:, j * LANES:(j + 1) * LANES]
            D[p, j, 0:24, :] = T[p, j, 0:24, :] - piece[0:24]
            D[p, j, 24:32, :] = (T[p, j, 24:32, :] - piece[24:32]) * not_last

    def update(p, acc):
        chunks = [D[p + 1, j, pl.ds(1, ROWS), :] for j in range(CHUNKS)]
        across = [D[p, j, pl.ds(1, ROWS), :] + D[p + 2, j, pl.ds(1, ROWS), :] for j in range(CHUNKS)]
        back = in_plane(chunks, across)
        for j in range(CHUNKS):
            old = S[p + 1, j, 8:32, :]
            defect = D[p + 1, j, 0:24, :]
            fresh = (wref[p, j] + (2.0 * old - defect) + back[j]) * recip[p, j]
            old_dual = dual[p, j]
            new_dual = fresh - old + defect
            primal = new_dual - old_dual
            S[p + 1, j, 8:32, :] = fresh
            dual[p, j] = new_dual
            square = primal * primal
            acc = acc + (square[0:8] + square[8:16] + square[16:24])
        return acc

    def record_primal(k, acc):
        record(k, 0, jnp.sum(acc, axis=(0, 1), keepdims=True))

    for copy in loads:
        copy.wait()

    @pl.when(s == 0)
    def _():
        for side in range(2):
            @pl.when(gets_from[side])
            def _():
                init_copy(side).wait_recv()

            @pl.when(sends_to[side])
            def _():
                init_copy(side).wait_send()
        for p in range(PLANES):
            own = [init_ref[p:p + 1, j * LANES:(j + 1) * LANES] for j in range(CHUNKS)]
            across = []
            for j in range(CHUNKS):
                cells = slice(j * LANES, (j + 1) * LANES)
                below = init_ref[p - 1:p, cells] if p > 0 else init_in[0, PLANES - 1:PLANES, cells]
                above = init_ref[p + 1:p + 2, cells] if p < PLANES - 1 else init_in[1, 0:1, cells]
                across.append(below + above)
            for j, value in enumerate(in_plane(own, across)):
                AS[p, j, 7:8, :] = value
        for p in range(PLANES):
            apply(p)
        part[...] = jnp.dot(lhs[:, PLANE:(PLANES + 1) * PLANE],
                            mat[1:PLANES + 1].reshape(PLANES * PLANE, WIDTH), preferred_element_type=F32)
        part_low[...] = part[...].astype(BF16)
        for d in range(1, groups):
            peer_copy(d, 0).start()

    def turn(p, carry):
        mat_t[p] = mat[p].T
        return carry

    lax.fori_loop(1, PLANES + 1, turn, 0)

    @pl.when(s == 0)
    def _():
        for d in range(1, groups):
            peer_copy(d, 0).wait_recv()
        inputs_low = solve(0, 0)
        for p in range(PLANES):
            drive(p + 1, inputs_low)
        for d in range(1, groups):
            peer_copy(d, 0).wait_send()

    acc = jnp.zeros((8, LANES), F32)
    for p in range(PLANES):
        acc = update(p, acc)
    record_primal(0, acc)
    for p in range(PLANES):
        apply(p)
    apply_outside(0)
    apply_outside(1)

    for piece in range(PIECES):
        for side in range(2):
            @pl.when(gets_from[side])
            def _():
                plane_copy(side, piece).wait_recv()
                pass_copy(side, piece, half).start()
    for side in range(2):
        @pl.when(gets_from[side])
        def _():
            for piece in range(PIECES):
                pass_copy(side, piece, PLANE // 2 - half).wait_recv()
            for piece in range(PIECES):
                pass_copy(side, piece, half).wait_send()

        @pl.when(sends_to[side])
        def _():
            for piece in range(PIECES):
                plane_copy(side, piece).wait_send()
    mat_t[0] = mat[0].T
    mat_t[PLANES + 1] = mat[PLANES + 1].T

    def iteration(k, carry):
        slot = lax.rem(k, 2)

        def start_cross():
            for i, (ds, dx) in enumerate(cross):
                @pl.when(inside(ds, dx))
                def _():
                    cross_copy(i, slot).start()

        if HALO_FIRST:
            start_cross()
        pulled = jnp.dot(lhs[...], mat[...].reshape((PLANES + 2) * PLANE, WIDTH), preferred_element_type=F32)
        part_low[...] = pulled.astype(BF16)
        for c in range(4):
            cells = slice(c * LANES, (c + 1) * LANES)
            tile[c:c + 1, :] = pulled[0:1, cells]
            tile[c + 4:c + 5, :] = pulled[24:25, cells]
        part[...] = pulled
        for d in range(groups):
            @pl.when(s < sections - 1)
            def _():
                tile_copy(1, d, slot).start()

            @pl.when(s > 0)
            def _():
                tile_copy(-1, d, slot).start()
        for d in range(1, groups):
            peer_copy(d, slot).start()
        if not HALO_FIRST:
            start_cross()

        for d in range(1, groups):
            peer_copy(d, slot).wait_recv()
        for d in range(groups):
            @pl.when(s > 0)
            def _():
                tile_copy(1, d, slot).wait_recv()

            @pl.when(s < sections - 1)
            def _():
                tile_copy(-1, d, slot).wait_recv()
        inputs_low = solve(k, slot)

        for i, (ds, dx) in enumerate(cross):
            @pl.when(inside(-ds, -dx))
            def _():
                cross_copy(i, slot).wait_recv()

        for j in range(CHUNKS):
            low = slice(j * LANES, (j + 1) * LANES)
            high_ = slice(PLANE + j * LANES, PLANE + (j + 1) * LANES)
            T[1, j] = T[1, j] + halo[slot, 0, :, high_].astype(F32)
            T[PLANES, j] = T[PLANES, j] + halo[slot, 1, :, low].astype(F32)
            T[0, j] = T[0, j] + halo[slot, 0, :, low].astype(F32)
            T[PLANES + 1, j] = T[PLANES + 1, j] + halo[slot, 1, :, high_].astype(F32)
            T[0, j, 24:25, :] += low0[slot, j:j + 1, :]
            T[PLANES + 1, j, 24:25, :] += high0[slot, j:j + 1, :]
            T[1, j, 0:1, :] += low24[slot, j:j + 1, :]
            T[PLANES, j, 0:1, :] += high24[slot, j:j + 1, :]
        for p in range(PLANES):
            for j in range(CHUNKS):
                T[p + 1, j, 0:1, :] += own24[slot, p, j:j + 1, :]
                T[p + 1, j, 24:25, :] += own0[slot, p, j:j + 1, :]

        for i, (ds, dx) in enumerate(cross):
            @pl.when(inside(ds, dx))
            def _():
                cross_copy(i, slot).wait_send()
        for d in range(1, groups):
            peer_copy(d, slot).wait_send()
        for d in range(groups):
            @pl.when(s < sections - 1)
            def _():
                tile_copy(1, d, slot).wait_send()

            @pl.when(s > 0)
            def _():
                tile_copy(-1, d, slot).wait_send()

        acc = jnp.zeros((8, LANES), F32)
        for q in range(PLANES + 2):
            drive(q, inputs_low)
            if q >= 2:
                acc = update(q - 2, acc)
            if q >= 3:
                apply(q - 3)
        apply(PLANES - 1)
        apply_outside(0)
        apply_outside(1)
        record_primal(k, acc)
        return carry

    lax.fori_loop(1, ITERS, iteration, 0)

    def first_copy(e):
        return pltpu.make_async_remote_copy(
            src_ref=hist, dst_ref=first_in.at[e - 1], send_sem=hist_send.at[e - 1], recv_sem=hist_recv.at[e - 1],
            device_id=pair_peer(e), device_id_type=MESH)

    def second_copy(e):
        i = pair_count - 2 + e
        return pltpu.make_async_remote_copy(
            src_ref=second, dst_ref=second_in.at[e - 1], send_sem=hist_send.at[i], recv_sem=hist_recv.at[i],
            device_id=column_peer(e), device_id_type=MESH)

    for e in range(1, pair_count):
        first_copy(e).start()

    for p in range(PLANES):
        for j in range(CHUNKS):
            ref_ref[j, pl.ds(p, ROWS, stride=PLANES), :] = S[p + 1, j, 8:32, :]
            weight_ref[j, pl.ds(p, ROWS, stride=PLANES), :] = dual[p, j]
    stores = [
        pltpu.make_async_copy(ref_ref, states_out, flat_sem.at[0, 0]),
        pltpu.make_async_copy(weight_ref, dual_out, flat_sem.at[1, 0]),
    ]
    for copy in stores:
        copy.start()
    boxed_out[...] = boxed[0:ROWS]

    for e in range(1, pair_count):
        first_copy(e).wait()
    total = hist[...]
    for e in range(1, pair_count):
        total = total + first_in[e - 1]
    second[...] = total
    for e in range(1, columns):
        second_copy(e).start()
    for e in range(1, columns):
        second_copy(e).wait()
    for e in range(1, columns):
        total = total + second_in[e - 1]
    column = lax.broadcasted_iota(jnp.int32, (16, LANES), 1)
    cells = float(ROWS * sections * GX * GY * GZ)
    inputs_count = float(ROWS * sections * WIDTH * groups)
    for copy in stores:
        copy.wait()
    hist_out[...] = jnp.sqrt(jnp.where(column == 0, total * (1.0 / cells), total * (1.0 / inputs_count)) + epsilon)


def deliver(states, boxed, dual_vars, record, states_out, boxed_out, dual_out, record_out, a, b, sem):
    loads, stores = [], []
    for i, (source, held, target) in enumerate(((states, a, states_out), (dual_vars, b, dual_out))):
        for j in range(CHUNKS):
            cells = pl.ds(j * LANES, LANES)
            loads.append(pltpu.make_async_copy(source.at[j], held.at[j], sem.at[i, j]))
            stores.append(pltpu.make_async_copy(held.at[j], target.at[:, cells], sem.at[2 + i, j]))
    for copy in loads:
        copy.start()
    boxed_out[...] = boxed[...]
    record_out[...] = record[0:ITERS, 0:2]
    for load, store in zip(loads, stores):
        load.wait()
        store.start()
    for copy in stores:
        copy.wait()


def solution(mesh):
    sections, groups = mesh.shape["section"], mesh.shape["state"]
    columns = sections // 2

    def local(initial_state, state_ref, state_weight, input_matrix, kkt_inverse, input_bound):
        vmem = pl.BlockSpec(memory_space=pltpu.VMEM)
        any_space = pl.BlockSpec(memory_space=pl.ANY)
        flat = (ROWS * PLANES, PLANE)
        chunked = (CHUNKS, ROWS * PLANES, LANES)
        V = pltpu.VMEM
        DMA = pltpu.SemaphoreType.DMA
        message_count = 8 + groups - 1 + 2 * groups
        compact = (CHUNKS, LANES)
        states, boxed, dual_vars, record = pl.pallas_call(
            functools.partial(kernel, sections, groups),
            out_shape=(
                jax.ShapeDtypeStruct(chunked, F32),
                jax.ShapeDtypeStruct((ROWS, WIDTH), F32),
                jax.ShapeDtypeStruct(chunked, F32),
                jax.ShapeDtypeStruct((16, LANES), F32),
            ),
            in_specs=[vmem, any_space, any_space, any_space, vmem, vmem],
            out_specs=(any_space, vmem, any_space, vmem),
            scratch_shapes=[
                V((CHUNKS, ROWS * PLANES, LANES), F32),
                V((CHUNKS, ROWS * PLANES, LANES), F32),
                V((PLANES + 2, PLANE, WIDTH), BF16),
                V((PLANES + 2, WIDTH, PLANE), BF16),
                V((PLANES + 2, CHUNKS, 40, LANES), F32),
                V((PLANES, CHUNKS, 40, LANES), F32),
                V((PLANES + 2, CHUNKS, 32, LANES), F32),
                V((PLANES + 2, CHUNKS, 32, LANES), F32),
                V((PLANES, CHUNKS, ROWS, LANES), F32),
                V((PLANES, CHUNKS, ROWS, LANES), F32),
                V((PLANES, CHUNKS, ROWS, LANES), F32),
                V((32, (PLANES + 2) * PLANE), BF16),
                V((2, 2, 32, 2 * PLANE), BF16),
                V((PLANES + 2, *compact), F32),
                V((PLANES, *compact), F32),
                V((2, PLANES, *compact), F32),
                V((2, *compact), F32),
                V((2, *compact), F32),
                V((2, PLANES, *compact), F32),
                V((2, *compact), F32),
                V((2, *compact), F32),
                V((32, WIDTH), F32),
                V((32, WIDTH), BF16),
                V((2, groups - 1, 32, WIDTH), BF16),
                V((2, PLANES, PLANE), F32),
                V(compact, F32),
                V((2, groups, *compact), F32),
                V((2, groups, *compact), F32),
                V((WIDTH, WIDTH), BF16),
                V((WIDTH, WIDTH), BF16),
                V((32, WIDTH), F32),
                V((32, WIDTH), F32),
                V((32, WIDTH), F32),
                V((16, LANES), F32),
                V((2 * groups - 1, 16, LANES), F32),
                V((16, LANES), F32),
                V((max(columns - 1, 1), 16, LANES), F32),
                DMA((PLANES,)),
                DMA((2, CHUNKS)),
                DMA((2, PIECES)),
                DMA((2, PIECES)),
                DMA((2, PIECES)),
                DMA((2, PIECES)),
                DMA((2,)),
                DMA((2,)),
                DMA((message_count,)),
                DMA((2, message_count)),
                DMA((2 * groups + columns,)),
                DMA((2 * groups + columns,)),
            ],
            compiler_params=pltpu.CompilerParams(
                collective_id=0, has_side_effects=True, vmem_limit_bytes=64000 * 1024),
        )(
            initial_state,
            state_ref.reshape(flat),
            state_weight.reshape(flat),
            input_matrix,
            kkt_inverse,
            input_bound.reshape(1, WIDTH),
        )
        states, boxed, dual_vars, record = pl.pallas_call(
            deliver,
            out_shape=(
                jax.ShapeDtypeStruct(flat, F32),
                jax.ShapeDtypeStruct((ROWS, WIDTH), F32),
                jax.ShapeDtypeStruct(flat, F32),
                jax.ShapeDtypeStruct((ITERS, 2), F32),
            ),
            in_specs=[any_space, vmem, any_space, vmem],
            out_specs=(any_space, vmem, any_space, vmem),
            scratch_shapes=[V(chunked, F32), V(chunked, F32), DMA((4, CHUNKS))],
        )(states, boxed, dual_vars, record)
        return (states.reshape(state_ref.shape), boxed, dual_vars.reshape(state_ref.shape), record)

    return jax.shard_map(
        local,
        mesh=mesh,
        in_specs=(
            P("state", None),
            P("section", "state", None),
            P("section", "state", None),
            P("state", None, None),
            P(),
            P(),
        ),
        out_specs=(P("section", "state", None), P("section", None), P("section", "state", None), P()),
        check_vma=False,
    )
```

time: 212 us -> 138 us (0.65)
  Pallas kernels: 204 us -> 136 us
  local copies, waits for them, and re-layouts: 6.83 us -> 1.34 us
    pallas_call x1, Pallas kernels: 204 us -> 132 us  [local(): pl.pallas_call(functools.partial(kernel, sections, groups), out_shape=(ja...]
    unnamed x3 -> x1, local copies, waits for them, and re-layouts: 5.6 us -> 1.34 us
    pallas_call x0 -> x1, Pallas kernels: none -> 3.82 us  [local(): pl.pallas_call(deliver, out_shape=(jax.ShapeDtypeStruct(flat, F32), jax.S...]
where the time goes in v2:
time: 138 us
  Pallas kernels  136 us (99%)
    pallas_call x1, Pallas kernels, local(): pl.pallas_call(functools.partial(kernel, sections, groups), out_shape=(ja...  132 us
    pallas_call x1, Pallas kernels, local(): pl.pallas_call(deliver, out_shape=(jax.ShapeDtypeStruct(flat, F32), jax.S...  3.82 us

profile of v2, /device:TPU:0, one launch (start us, length us, event | category | flops | bytes accessed | tf_op | source)
XLA Modules:
  0.0 137.6 jit_solution(8890033748349570823)
XLA Ops:
  0.6 131.8 %shard_map.93 = (f32[8,192,128]{2,1,0:T(8,128)}, f32[24,512]{1,0:T(8,128)}, f32[8,192,128]{2,1,0:T(8,128)}, f32[16,128]{1,0:T(8,128)}) custom-call(f32[8,1024]{1,0:T(8,128)} %init_ref.1, f32[192,1024]{1,0:T(8,128)} %bitcast.5, f32[192,1024]{1,0:T(8,128)} %bitcast.6, bf16[8,1024,512]{2,1,0:T(8,128)(2,1)} %matrix_hbm.1, f32[512,512]{1,0:T(8,128)} %kkt_ref.1, ...), custom_call_target="tpu_custom_call" | custom-call | tf_op jit(solution)/shard_map/pallas_call | solution.py:556
  132.5 3.8 %shard_map.94 = (f32[192,1024]{1,0:T(8,128)}, f32[24,512]{1,0:T(8,128)}, f32[192,1024]{1,0:T(8,128)}, f32[10,2]{1,0:T(8,128)}) custom-call(f32[8,192,128]{2,1,0:T(8,128)} %get-tuple-element.12.states, f32[24,512]{1,0:T(8,128)} %get-tuple-element.13.boxed, f32[8,192,128]{2,1,0:T(8,128)} %get-tuple-element.14.dual_vars, f32[16,128]{1,0:T(8,128)} %get-tuple-element.15.record), custom_call_target="tpu_custom_call" | custom-call | tf_op jit(solution)/shard_map/pallas_call | solution.py:627
  136.3 1.3 copy.10

commit v3 on v2

--- a/solution.py
+++ b/solution.py
@@ -11,8 +11,8 @@
 GY = 32
 GZ = 32
 ITERS = 10
-PIECES = 4
-HALO_FIRST = True
+BLOCKS = 8
+FOLD = 1536
 PLANES = 8
 CHUNKS = 8
 ROWS = 24
@@ -26,30 +26,28 @@
 BF16 = jnp.bfloat16
 
 
-def in_plane(chunks, across):
+def in_plane(chunk, across):
     lane = lax.broadcasted_iota(jnp.int32, (1, LANES), 1)
     along = lane % GZ
-    down = [pltpu.roll(c, GZ, 1) for c in chunks]
-    up = [pltpu.roll(c, LANES - GZ, 1) for c in chunks]
-    out = []
-    for j, c in enumerate(chunks):
-        below = down[j - 1] if j > 0 else 0.0
-        above = up[j + 1] if j < CHUNKS - 1 else 0.0
-        y_sum = jnp.where(lane < GZ, below, down[j]) + jnp.where(lane >= LANES - GZ, above, up[j])
-        lower = jnp.where(along > 0, pltpu.roll(c, 1, 1), 0.0)
-        upper = jnp.where(along < GZ - 1, pltpu.roll(c, LANES - 1, 1), 0.0)
-        total = y_sum + lower + upper
-        if across is not None:
-            total = total + across[j]
-        out.append((1.0 - 6.0 * diffusion) * c + diffusion * total)
-    return out
-
-
-def kernel(sections, groups, init_ref, ref_hbm, weight_hbm, matrix_hbm, kkt_ref, bound_ref,
+    here = chunk(0)
+    before = None
+    for j in range(CHUNKS):
+        after = chunk(j + 1) if j < CHUNKS - 1 else None
+        below = pltpu.roll(before, GZ, 1) if j > 0 else 0.0
+        above = pltpu.roll(after, LANES - GZ, 1) if j < CHUNKS - 1 else 0.0
+        y_sum = jnp.where(lane < GZ, below, pltpu.roll(here, GZ, 1)) + jnp.where(
+            lane >= LANES - GZ, above, pltpu.roll(here, LANES - GZ, 1))
+        lower = jnp.where(along > 0, pltpu.roll(here, 1, 1), 0.0)
+        upper = jnp.where(along < GZ - 1, pltpu.roll(here, LANES - 1, 1), 0.0)
+        yield j, here, (1.0 - 6.0 * diffusion) * here + diffusion * ((y_sum + lower) + (upper + across(j)))
+        before, here = here, after
+
+
+def kernel(sections, groups, init_ref, ref_hbm, weight_hbm, matrix_hbm, kkt_hbm, bound_ref,
            states_out, boxed_out, dual_out, hist_out,
-           ref_ref, weight_ref, mat, mat_t, S, AS, T, D, dual, wref, recip, lhs, halo,
+           ref_ref, weight_ref, kkt_ref, mat, mat_t, S, AS, T, D, dual, wref, recip, lhs, halo,
            send24, send0, own24, low24, high24, own0, low0, high0,
-           part, part_low, part_in, init_in, tile, tile_prev, tile_next, k_high, k_low, pul, boxed, scaled,
+           fold, edge24, part, part_low, part_in, init_in, tile, tile_prev, tile_same, tile_next, k_high, k_low, pul, boxed, scaled,
            hist, first_in, second, second_in,
            load_sem, flat_sem, halo_send, halo_recv, pass_send, pass_recv, init_send, init_recv, send_sem, recv_sem, hist_send, hist_recv):
     s = lax.axis_index("section")
@@ -72,7 +70,7 @@
         return (lax.rem(s // 2 + e, columns) * 2 + lax.rem(s, 2), x)
 
     zeros = lambda ref: ref.__setitem__(Ellipsis, jnp.zeros(ref.shape, ref.dtype))
-    for ref in (halo, own24, low24, high24, own0, low0, high0, init_in):
+    for ref in (halo, own24, low24, high24, own0, low0, high0, init_in, edge24):
         zeros(ref)
 
     barrier = pltpu.get_barrier_semaphore()
@@ -99,7 +97,8 @@
         cells = pl.ds(j * LANES, LANES)
         flat_loads.append(pltpu.make_async_copy(weight_hbm.at[:, cells], weight_ref.at[j], flat_sem.at[0, j]))
         flat_loads.append(pltpu.make_async_copy(ref_hbm.at[:, cells], ref_ref.at[j], flat_sem.at[1, j]))
-    for copy in flat_loads + loads:
+    kkt_load = pltpu.make_async_copy(kkt_hbm, kkt_ref, load_sem.at[PLANES])
+    for copy in flat_loads + [kkt_load] + loads:
         copy.start()
 
     for ref in (AS, T, D, dual, S, boxed, scaled, hist):
@@ -121,22 +120,24 @@
     )
     pl.semaphore_wait(barrier, neighbours)
 
-    half = lax.rem(s, 2) * (PLANE // 2)
     twin = s + 1 - 2 * lax.rem(s, 2)
-    depth = PLANE // 2 // PIECES
+    depth = PLANE // BLOCKS
+
+    def mine(block):
+        return lax.rem(s, 2) == jnp.where(s < 2, 1, block // (BLOCKS // 2))
 
     def plane_copy(side, piece):
         source = 0 if side == 0 else PLANES - 1
         target = PLANES + 1 if side == 0 else 0
-        rows = pl.ds(pl.multiple_of(half + piece * depth, depth), depth)
+        rows = pl.ds(piece * depth, depth)
         return pltpu.make_async_remote_copy(
             src_ref=matrix_hbm.at[source, rows], dst_ref=mat.at[target, rows],
             send_sem=halo_send.at[side, piece], recv_sem=halo_recv.at[side, piece],
             device_id=(s, x - 1 if side == 0 else x + 1), device_id_type=MESH)
 
-    def pass_copy(side, piece, start):
+    def pass_copy(side, piece):
         target = PLANES + 1 if side == 0 else 0
-        rows = pl.ds(pl.multiple_of(start + piece * depth, depth), depth)
+        rows = pl.ds(piece * depth, depth)
         return pltpu.make_async_remote_copy(
             src_ref=mat.at[target, rows], dst_ref=mat.at[target, rows],
             send_sem=pass_send.at[side, piece], recv_sem=pass_recv.at[side, piece],
@@ -155,11 +156,13 @@
         def _():
             init_copy(side).start()
 
-        @pl.when(sends_to[side])
-        def _():
-            for piece in range(PIECES):
+    for piece in range(BLOCKS):
+        for side in range(2):
+            @pl.when(sends_to[side] & mine(piece))
+            def _():
                 plane_copy(side, piece).start()
 
+    kkt_load.wait()
     kkt = kkt_ref[...]
     high = kkt.astype(BF16)
     k_high[...] = high
@@ -176,20 +179,21 @@
     penalty = float(GX * GY * GZ) / WIDTH
     not_last = jnp.where(s < sections - 1, 1.0, 0.0).astype(F32)
     has_side = (jnp.where(x > 0, 1.0, 0.0).astype(F32), jnp.where(x < groups - 1, 1.0, 0.0).astype(F32))
-    cross = [(0, -1), (0, 1), (1, 0), (1, 1), (1, -1), (-1, 0), (-1, 1), (-1, -1)]
+    cross = [(0, -1), (0, 1), (1, 0), (1, 1), (1, -1), (-1, 0), (-1, 1), (-1, -1), (0, -1), (0, 1)]
     base_index = len(cross)
 
     def messages(slot):
-        side = 2 * PLANE
         return [
-            (lhs.at[:, pl.ds(0, side)], halo.at[slot, 1]),
-            (lhs.at[:, pl.ds(PLANES * PLANE, side)], halo.at[slot, 0]),
+            (fold.at[0], halo.at[slot, 1]),
+            (fold.at[1], halo.at[slot, 0]),
             (send24.at[pl.ds(1, PLANES)], own24.at[slot]),
             (send24.at[PLANES + 1], low24.at[slot]),
             (send24.at[0], high24.at[slot]),
             (send0, own0.at[slot]),
             (send0.at[PLANES - 1], low0.at[slot]),
             (send0.at[0], high0.at[slot]),
+            (send24.at[pl.ds(0, 2)], edge24.at[slot, 1]),
+            (send24.at[pl.ds(PLANES, 2)], edge24.at[slot, 0]),
         ]
 
     def cross_copy(i, slot):
@@ -206,19 +210,33 @@
             recv_sem=recv_sem.at[slot, i], device_id=(s, rotated(d)), device_id_type=MESH)
 
     def tile_copy(ds, d, slot):
-        i = base_index + groups - 1 + (groups if ds > 0 else 0) + d
-        target = tile_prev if ds > 0 else tile_next
+        i = base_index + groups - 1 + groups * (ds + 1) + d
+        target = (tile_next, tile_same, tile_prev)[ds + 1]
         return pltpu.make_async_remote_copy(
-            src_ref=tile, dst_ref=target.at[slot, d], send_sem=send_sem.at[i],
+            src_ref=tile, dst_ref=target.at[slot, d - 1 if ds == 0 else d], send_sem=send_sem.at[i],
             recv_sem=recv_sem.at[slot, i], device_id=(s + ds, rotated(d)), device_id_type=MESH)
 
+    def folded(side, outside, full):
+        base = (0 if outside else FOLD) if side == 0 else (FOLD if outside else 0)
+        for j in range(CHUNKS):
+            fold[side, :, base + j * LANES:base + (j + 1) * LANES] = full[j][0:16].astype(BF16)
+        for j in range(CHUNKS // 2):
+            pair = jnp.concatenate([full[j][16:24], full[j + CHUNKS // 2][16:24]], 0)
+            fold[side, :, base + PLANE + j * LANES:base + PLANE + (j + 1) * LANES] = pair.astype(BF16)
+
+    def unfolded(slot, side, base, j):
+        top = halo[slot, side, :, base + j * LANES:base + (j + 1) * LANES].astype(F32)
+        i = j % (CHUNKS // 2)
+        pair = halo[slot, side, :, base + PLANE + i * LANES:base + PLANE + (i + 1) * LANES].astype(F32)
+        start = 8 * (j // (CHUNKS // 2))
+        return jnp.concatenate([top, pair[start:start + 8]], 0)
+
     def apply(p):
-        chunks = [S[p + 1, j, 8:32, :] for j in range(CHUNKS)]
-        across = [S[p, j, 8:32, :] + S[p + 2, j, 8:32, :] for j in range(CHUNKS)]
-        for j, value in enumerate(in_plane(chunks, across)):
+        bodies = []
+        moved = in_plane(lambda j: S[p + 1, j, 8:32, :], lambda j: S[p, j, 8:32, :] + S[p + 2, j, 8:32, :])
+        for j, here, value in moved:
             AS[p, j, 8:32, :] = value
-        for j in range(CHUNKS):
-            body = chunks[j] + dual[p, j] - AS[p, j, pl.ds(7, ROWS), :]
+            body = here + dual[p, j] - AS[p, j, pl.ds(7, ROWS), :]
             tail = -AS[p, j, pl.ds(31, 8), :]
             T[p + 1, j, 0:24, :] = body
             T[p + 1, j, 24:32, :] = tail
@@ -226,20 +244,39 @@
                 [body, tail], 0).astype(BF16)
             send24[p + 1, j:j + 1, :] = tail[0:1]
             send0[p, j:j + 1, :] = body[0:1]
+            if p in (0, PLANES - 1):
+                bodies.append(body)
+        if p in (0, PLANES - 1):
+            folded(0 if p == 0 else 1, False, bodies)
 
     def apply_outside(side):
         p, q = ((0, 1), (PLANES + 1, PLANES))[side]
+        bodies = []
         for j in range(CHUNKS):
             full = (-diffusion * has_side[side]) * S[q, j, pl.ds(7, 32), :]
             T[p, j] = full
             lhs[:, p * PLANE + j * LANES:p * PLANE + (j + 1) * LANES] = full.astype(BF16)
             send24[p, j:j + 1, :] = full[24:25]
+            bodies.append(full)
+        folded(side, True, bodies)
 
     def solve(k, slot):
         total = part[...]
+        top, tail, low = total[0:16], total[16:24], total[24:32]
         for d in range(1, groups):
-            total = total + part_in[slot, d - 1].astype(F32)
-        pul[...] = total + penalty * (boxed[...] - scaled[...])
+            piece = part_in[slot, d - 1].astype(F32)
+            top = top + piece[:, 0:WIDTH]
+            tail = tail + jnp.concatenate([piece[0:8, WIDTH:], piece[8:16, WIDTH:]], 1)
+        pul[...] = jnp.concatenate([top, tail, low], 0) + penalty * (boxed[...] - scaled[...])
+
+        @pl.when(k > 0)
+        def _():
+            incoming = tile_same[slot, 0]
+            for d in range(2, groups):
+                incoming = incoming + tile_same[slot, d - 1]
+            for c in range(4):
+                cells = slice(c * LANES, (c + 1) * LANES)
+                pul[24:25, cells] += incoming[c + 4:c + 5]
 
         @pl.when((s > 0) & (k > 0))
         def _():
@@ -273,26 +310,31 @@
         record(k, 1, gap_sum)
         return inputs.astype(BF16)
 
+    def narrow(value):
+        part_low[:, 0:WIDTH] = value[0:16].astype(BF16)
+        half = WIDTH // 2
+        part_low[:, WIDTH:] = jnp.concatenate([value[16:24, 0:half], value[16:24, half:]], 0).astype(BF16)
+
     def record(k, kind, value):
-        row = lax.broadcasted_iota(jnp.int32, (16, LANES), 0)
-        column = lax.broadcasted_iota(jnp.int32, (16, LANES), 1)
-        hist[...] += jnp.where((column == kind) & (row == k), value, 0.0)
+        row = lax.broadcasted_iota(jnp.int32, (8, LANES), 0)
+        column = lax.broadcasted_iota(jnp.int32, (8, LANES), 1)
+        hist[...] += jnp.where((row == kind) & (column == k), value, 0.0)
 
     def drive(p, inputs_low):
-        driven = jnp.dot(inputs_low, mat_t[p], preferred_element_type=F32)
-        for j in range(CHUNKS):
-            piece = driven[:, j * LANES:(j + 1) * LANES]
-            D[p, j, 0:24, :] = T[p, j, 0:24, :] - piece[0:24]
-            D[p, j, 24:32, :] = (T[p, j, 24:32, :] - piece[24:32]) * not_last
+        for i in range(PLANE // 256):
+            driven = jnp.dot(inputs_low, mat_t[p, :, i * 256:(i + 1) * 256], preferred_element_type=F32)
+            for j in (2 * i, 2 * i + 1):
+                piece = driven[:, (j % 2) * LANES:(j % 2 + 1) * LANES]
+                D[p, j, 0:24, :] = T[p, j, 0:24, :] - piece[0:24]
+                D[p, j, 24:32, :] = (T[p, j, 24:32, :] - piece[24:32]) * not_last
 
     def update(p, acc):
-        chunks = [D[p + 1, j, pl.ds(1, ROWS), :] for j in range(CHUNKS)]
-        across = [D[p, j, pl.ds(1, ROWS), :] + D[p + 2, j, pl.ds(1, ROWS), :] for j in range(CHUNKS)]
-        back = in_plane(chunks, across)
-        for j in range(CHUNKS):
+        back = in_plane(lambda j: D[p + 1, j, pl.ds(1, ROWS), :],
+                        lambda j: D[p, j, pl.ds(1, ROWS), :] + D[p + 2, j, pl.ds(1, ROWS), :])
+        for j, _, value in back:
             old = S[p + 1, j, 8:32, :]
             defect = D[p + 1, j, 0:24, :]
-            fresh = (wref[p, j] + (2.0 * old - defect) + back[j]) * recip[p, j]
+            fresh = (wref[p, j] + (2.0 * old - defect) + value) * recip[p, j]
             old_dual = dual[p, j]
             new_dual = fresh - old + defect
             primal = new_dual - old_dual
@@ -319,20 +361,22 @@
             def _():
                 init_copy(side).wait_send()
         for p in range(PLANES):
-            own = [init_ref[p:p + 1, j * LANES:(j + 1) * LANES] for j in range(CHUNKS)]
-            across = []
-            for j in range(CHUNKS):
+            def own(j):
+                return init_ref[p:p + 1, j * LANES:(j + 1) * LANES]
+
+            def beside(j):
                 cells = slice(j * LANES, (j + 1) * LANES)
                 below = init_ref[p - 1:p, cells] if p > 0 else init_in[0, PLANES - 1:PLANES, cells]
                 above = init_ref[p + 1:p + 2, cells] if p < PLANES - 1 else init_in[1, 0:1, cells]
-                across.append(below + above)
-            for j, value in enumerate(in_plane(own, across)):
+                return below + above
+
+            for j, _, value in in_plane(own, beside):
                 AS[p, j, 7:8, :] = value
         for p in range(PLANES):
             apply(p)
         part[...] = jnp.dot(lhs[:, PLANE:(PLANES + 1) * PLANE],
                             mat[1:PLANES + 1].reshape(PLANES * PLANE, WIDTH), preferred_element_type=F32)
-        part_low[...] = part[...].astype(BF16)
+        narrow(part[...])
         for d in range(1, groups):
             peer_copy(d, 0).start()
 
@@ -361,40 +405,47 @@
     apply_outside(0)
     apply_outside(1)
 
-    for piece in range(PIECES):
+    for piece in range(BLOCKS):
         for side in range(2):
-            @pl.when(gets_from[side])
+            @pl.when(gets_from[side] & mine(piece))
             def _():
                 plane_copy(side, piece).wait_recv()
-                pass_copy(side, piece, half).start()
-    for side in range(2):
-        @pl.when(gets_from[side])
-        def _():
-            for piece in range(PIECES):
-                pass_copy(side, piece, PLANE // 2 - half).wait_recv()
-            for piece in range(PIECES):
-                pass_copy(side, piece, half).wait_send()
-
-        @pl.when(sends_to[side])
-        def _():
-            for piece in range(PIECES):
+                pass_copy(side, piece).start()
+    for piece in range(BLOCKS):
+        for side in range(2):
+            @pl.when(gets_from[side] & jnp.logical_not(mine(piece)))
+            def _():
+                pass_copy(side, piece).wait_recv()
+
+            @pl.when(gets_from[side] & mine(piece))
+            def _():
+                pass_copy(side, piece).wait_send()
+
+            @pl.when(sends_to[side] & mine(piece))
+            def _():
                 plane_copy(side, piece).wait_send()
     mat_t[0] = mat[0].T
     mat_t[PLANES + 1] = mat[PLANES + 1].T
 
+    early = 1
+
+    def start_cross(i, slot):
+        ds, dx = cross[i]
+
+        @pl.when(inside(ds, dx))
+        def _():
+            cross_copy(i, slot).start()
+
+    start_cross(early, 1)
+
     def iteration(k, carry):
         slot = lax.rem(k, 2)
-
-        def start_cross():
-            for i, (ds, dx) in enumerate(cross):
-                @pl.when(inside(ds, dx))
-                def _():
-                    cross_copy(i, slot).start()
-
-        if HALO_FIRST:
-            start_cross()
+        for i in range(len(cross)):
+            if i != early:
+                start_cross(i, slot)
+
         pulled = jnp.dot(lhs[...], mat[...].reshape((PLANES + 2) * PLANE, WIDTH), preferred_element_type=F32)
-        part_low[...] = pulled.astype(BF16)
+        narrow(pulled)
         for c in range(4):
             cells = slice(c * LANES, (c + 1) * LANES)
             tile[c:c + 1, :] = pulled[0:1, cells]
@@ -408,22 +459,9 @@
             @pl.when(s > 0)
             def _():
                 tile_copy(-1, d, slot).start()
-        for d in range(1, groups):
+        for d in (2, 1, 3):
             peer_copy(d, slot).start()
-        if not HALO_FIRST:
-            start_cross()
-
-        for d in range(1, groups):
-            peer_copy(d, slot).wait_recv()
-        for d in range(groups):
-            @pl.when(s > 0)
-            def _():
-                tile_copy(1, d, slot).wait_recv()
-
-            @pl.when(s < sections - 1)
-            def _():
-                tile_copy(-1, d, slot).wait_recv()
-        inputs_low = solve(k, slot)
+            tile_copy(0, d, slot).start()
 
         for i, (ds, dx) in enumerate(cross):
             @pl.when(inside(-ds, -dx))
@@ -431,14 +469,14 @@
                 cross_copy(i, slot).wait_recv()
 
         for j in range(CHUNKS):
-            low = slice(j * LANES, (j + 1) * LANES)
-            high_ = slice(PLANE + j * LANES, PLANE + (j + 1) * LANES)
-            T[1, j] = T[1, j] + halo[slot, 0, :, high_].astype(F32)
-            T[PLANES, j] = T[PLANES, j] + halo[slot, 1, :, low].astype(F32)
-            T[0, j] = T[0, j] + halo[slot, 0, :, low].astype(F32)
-            T[PLANES + 1, j] = T[PLANES + 1, j] + halo[slot, 1, :, high_].astype(F32)
-            T[0, j, 24:25, :] += low0[slot, j:j + 1, :]
-            T[PLANES + 1, j, 24:25, :] += high0[slot, j:j + 1, :]
+            T[0, j, 0:24, :] += unfolded(slot, 0, 0, j)
+            T[1, j, 0:24, :] += unfolded(slot, 0, FOLD, j)
+            T[PLANES, j, 0:24, :] += unfolded(slot, 1, 0, j)
+            T[PLANES + 1, j, 0:24, :] += unfolded(slot, 1, FOLD, j)
+            T[0, j, 24:25, :] += low0[slot, j:j + 1, :] + edge24[slot, 0, 0, j:j + 1, :]
+            T[1, j, 24:25, :] += edge24[slot, 0, 1, j:j + 1, :]
+            T[PLANES, j, 24:25, :] += edge24[slot, 1, 0, j:j + 1, :]
+            T[PLANES + 1, j, 24:25, :] += high0[slot, j:j + 1, :] + edge24[slot, 1, 1, j:j + 1, :]
             T[1, j, 0:1, :] += low24[slot, j:j + 1, :]
             T[PLANES, j, 0:1, :] += high24[slot, j:j + 1, :]
         for p in range(PLANES):
@@ -450,8 +488,40 @@
             @pl.when(inside(ds, dx))
             def _():
                 cross_copy(i, slot).wait_send()
+
+        for d in range(1, groups):
+            peer_copy(d, slot).wait_recv()
+            tile_copy(0, d, slot).wait_recv()
+        for d in range(groups):
+            @pl.when(s > 0)
+            def _():
+                tile_copy(1, d, slot).wait_recv()
+
+            @pl.when(s < sections - 1)
+            def _():
+                tile_copy(-1, d, slot).wait_recv()
+        inputs_low = solve(k, slot)
+
+        acc = jnp.zeros((8, LANES), F32)
+        for q in range(PLANES + 1, -1, -1):
+            drive(q, inputs_low)
+            if q < PLANES:
+                acc = update(q, acc)
+            if q < PLANES - 1:
+                apply(q + 1)
+            if q == PLANES - 2:
+                apply_outside(1)
+
+                @pl.when(k < ITERS - 1)
+                def _():
+                    start_cross(early, 1 - slot)
+        apply(0)
+        apply_outside(0)
+        record_primal(k, acc)
+
         for d in range(1, groups):
             peer_copy(d, slot).wait_send()
+            tile_copy(0, d, slot).wait_send()
         for d in range(groups):
             @pl.when(s < sections - 1)
             def _():
@@ -460,18 +530,6 @@
             @pl.when(s > 0)
             def _():
                 tile_copy(-1, d, slot).wait_send()
-
-        acc = jnp.zeros((8, LANES), F32)
-        for q in range(PLANES + 2):
-            drive(q, inputs_low)
-            if q >= 2:
-                acc = update(q - 2, acc)
-            if q >= 3:
-                apply(q - 3)
-        apply(PLANES - 1)
-        apply_outside(0)
-        apply_outside(1)
-        record_primal(k, acc)
         return carry
 
     lax.fori_loop(1, ITERS, iteration, 0)
@@ -514,12 +572,12 @@
         second_copy(e).wait()
     for e in range(1, columns):
         total = total + second_in[e - 1]
-    column = lax.broadcasted_iota(jnp.int32, (16, LANES), 1)
+    row = lax.broadcasted_iota(jnp.int32, (8, LANES), 0)
     cells = float(ROWS * sections * GX * GY * GZ)
     inputs_count = float(ROWS * sections * WIDTH * groups)
     for copy in stores:
         copy.wait()
-    hist_out[...] = jnp.sqrt(jnp.where(column == 0, total * (1.0 / cells), total * (1.0 / inputs_count)) + epsilon)
+    hist_out[...] = jnp.sqrt(jnp.where(row == 0, total * (1.0 / cells), total * (1.0 / inputs_count)) + epsilon)
 
 
 def deliver(states, boxed, dual_vars, record, states_out, boxed_out, dual_out, record_out, a, b, sem):
@@ -532,7 +590,7 @@
     for copy in loads:
         copy.start()
     boxed_out[...] = boxed[...]
-    record_out[...] = record[0:ITERS, 0:2]
+    record_out[...] = record[0:2, 0:ITERS]
     for load, store in zip(loads, stores):
         load.wait()
         store.start()
@@ -551,7 +609,7 @@
         chunked = (CHUNKS, ROWS * PLANES, LANES)
         V = pltpu.VMEM
         DMA = pltpu.SemaphoreType.DMA
-        message_count = 8 + groups - 1 + 2 * groups
+        message_count = 10 + groups - 1 + 3 * groups
         compact = (CHUNKS, LANES)
         states, boxed, dual_vars, record = pl.pallas_call(
             functools.partial(kernel, sections, groups),
@@ -559,13 +617,14 @@
                 jax.ShapeDtypeStruct(chunked, F32),
                 jax.ShapeDtypeStruct((ROWS, WIDTH), F32),
                 jax.ShapeDtypeStruct(chunked, F32),
-                jax.ShapeDtypeStruct((16, LANES), F32),
+                jax.ShapeDtypeStruct((8, LANES), F32),
             ),
-            in_specs=[vmem, any_space, any_space, any_space, vmem, vmem],
+            in_specs=[vmem, any_space, any_space, any_space, any_space, vmem],
             out_specs=(any_space, vmem, any_space, vmem),
             scratch_shapes=[
                 V((CHUNKS, ROWS * PLANES, LANES), F32),
                 V((CHUNKS, ROWS * PLANES, LANES), F32),
+                V((WIDTH, WIDTH), F32),
                 V((PLANES + 2, PLANE, WIDTH), BF16),
                 V((PLANES + 2, WIDTH, PLANE), BF16),
                 V((PLANES + 2, CHUNKS, 40, LANES), F32),
@@ -576,7 +635,7 @@
                 V((PLANES, CHUNKS, ROWS, LANES), F32),
                 V((PLANES, CHUNKS, ROWS, LANES), F32),
                 V((32, (PLANES + 2) * PLANE), BF16),
-                V((2, 2, 32, 2 * PLANE), BF16),
+                V((2, 2, 16, 2 * FOLD), BF16),
                 V((PLANES + 2, *compact), F32),
                 V((PLANES, *compact), F32),
                 V((2, PLANES, *compact), F32),
@@ -585,28 +644,31 @@
                 V((2, PLANES, *compact), F32),
                 V((2, *compact), F32),
                 V((2, *compact), F32),
+                V((2, 16, 2 * FOLD), BF16),
+                V((2, 2, 2, *compact), F32),
                 V((32, WIDTH), F32),
-                V((32, WIDTH), BF16),
-                V((2, groups - 1, 32, WIDTH), BF16),
+                V((16, WIDTH + WIDTH // 2), BF16),
+                V((2, groups - 1, 16, WIDTH + WIDTH // 2), BF16),
                 V((2, PLANES, PLANE), F32),
                 V(compact, F32),
                 V((2, groups, *compact), F32),
+                V((2, groups - 1, *compact), F32),
                 V((2, groups, *compact), F32),
                 V((WIDTH, WIDTH), BF16),
                 V((WIDTH, WIDTH), BF16),
                 V((32, WIDTH), F32),
                 V((32, WIDTH), F32),
                 V((32, WIDTH), F32),
-                V((16, LANES), F32),
-                V((2 * groups - 1, 16, LANES), F32),
-                V((16, LANES), F32),
-                V((max(columns - 1, 1), 16, LANES), F32),
-                DMA((PLANES,)),
+                V(compact, F32),
+                V((2 * groups - 1, *compact), F32),
+                V(compact, F32),
+                V((max(columns - 1, 1), *compact), F32),
+                DMA((PLANES + 1,)),
                 DMA((2, CHUNKS)),
-                DMA((2, PIECES)),
-                DMA((2, PIECES)),
-                DMA((2, PIECES)),
-                DMA((2, PIECES)),
+                DMA((2, BLOCKS)),
+                DMA((2, BLOCKS)),
+                DMA((2, BLOCKS)),
+                DMA((2, BLOCKS)),
                 DMA((2,)),
                 DMA((2,)),
                 DMA((message_count,)),
@@ -630,13 +692,13 @@
                 jax.ShapeDtypeStruct(flat, F32),
                 jax.ShapeDtypeStruct((ROWS, WIDTH), F32),
                 jax.ShapeDtypeStruct(flat, F32),
-                jax.ShapeDtypeStruct((ITERS, 2), F32),
+                jax.ShapeDtypeStruct((2, ITERS), F32),
             ),
             in_specs=[any_space, vmem, any_space, vmem],
             out_specs=(any_space, vmem, any_space, vmem),
             scratch_shapes=[V(chunked, F32), V(chunked, F32), DMA((4, CHUNKS))],
         )(states, boxed, dual_vars, record)
-        return (states.reshape(state_ref.shape), boxed, dual_vars.reshape(state_ref.shape), record)
+        return (states.reshape(state_ref.shape), boxed, dual_vars.reshape(state_ref.shape), record.T)
 
     return jax.shard_map(
         local,

time: 138 us -> 129 us (0.935)
  Pallas kernels: 136 us -> 128 us
    pallas_call x1, Pallas kernels: 132 us -> 124 us  [local(): pl.pallas_call(functools.partial(kernel, sections, groups), out_shape=(ja...]
where the time goes in v3:
time: 129 us
  Pallas kernels  128 us (99%)
    pallas_call x1, Pallas kernels, local(): pl.pallas_call(functools.partial(kernel, sections, groups), out_shape=(ja...  124 us
    pallas_call x1, Pallas kernels, local(): pl.pallas_call(deliver, out_shape=(jax.ShapeDtypeStruct(flat, F32), jax.S...  3.82 us

profile of v3, /device:TPU:0, one launch (start us, length us, event | category | flops | bytes accessed | tf_op | source)
XLA Modules:
  0.0 128.7 jit_solution(15632899736318218985)
XLA Ops:
  0.6 124.2 %shard_map.93 = (f32[8,192,128]{2,1,0:T(8,128)}, f32[24,512]{1,0:T(8,128)}, f32[8,192,128]{2,1,0:T(8,128)}, f32[8,128]{1,0:T(8,128)}) custom-call(f32[8,1024]{1,0:T(8,128)} %init_ref.1, f32[192,1024]{1,0:T(8,128)} %bitcast.6, f32[192,1024]{1,0:T(8,128)} %bitcast.7, bf16[8,1024,512]{2,1,0:T(8,128)(2,1)} %matrix_hbm.1, f32[512,512]{1,0:T(8,128)} %kkt_hbm.1, ...), custom_call_target="tpu_custom_call" | custom-call | tf_op jit(solution)/shard_map/pallas_call | solution.py:614
  124.8 3.8 %shard_map.94 = (f32[192,1024]{1,0:T(8,128)}, f32[24,512]{1,0:T(8,128)}, f32[192,1024]{1,0:T(8,128)}, f32[2,10]{1,0:T(2,128)}) custom-call(f32[8,192,128]{2,1,0:T(8,128)} %get-tuple-element.12.states, f32[24,512]{1,0:T(8,128)} %get-tuple-element.13.boxed, f32[8,192,128]{2,1,0:T(8,128)} %get-tuple-element.14.dual_vars, f32[8,128]{1,0:T(8,128)} %get-tuple-element.15.record), custom_call_target="tpu_custom_call" | custom-call | tf_op jit(solution)/shard_map/pallas_call | solution.py:689
